TPU v7x, 256 devices: a whole 4x4x8 slice. The times are simulated.
256 devices in a mesh: seq: 64 (over x, z, core), head: 4 (over y).
Axes of the slice: x: 4, y: 4, z: 8, core: 2. Of those that a mesh axis runs over, the one named last changes fastest.
Arguments:
- queries: bfloat16 [32768, 1024], P('seq', 'head'), may hold values from -6 to 6
- key_vectors: bfloat16 [32768, 1024], P('seq', 'head'), may hold values from -6 to 6
- values: bfloat16 [32768, 2048], P('seq', 'head'), may hold values from -6 to 6
- log_gate: bfloat16 [32768, 1024], P('seq', 'head'), may hold values from -1.6 to 0, as said below
- out_gate: bfloat16 [32768, 2048], P('seq', 'head'), may hold values from -6 to 6
- norm_gain: float32 [2048], P('head'), may hold values from 0.5 to 1.5
- out_weight: bfloat16 [2048, 2048], P('head'), may hold values from -0.1875 to 0.1875
Outputs:
- mixed: bfloat16 [32768, 2048], P('seq', 'head')
Inputs may be any that keep to these rules, and one draw needn't show every extreme that they name: `log_gate`: every entry is below zero.
All inputs are finite; a program needn't handle non-finite values.
Results may differ from a plain program's by a relative error of at most 0.017.
Values may be sent and summed in bfloat16 or wider, within the bound.
No kernel may reach another device: no remote copies, remote signals or barrier semaphores. Data moves between devices by JAX's collectives and lax.ppermute only.
A program may use at most 128 MiB of HBM per device.

v0:
```python
import jax
import jax.numpy as jnp
from jax import lax
from jax.sharding import Mesh
from jax.sharding import PartitionSpec as P

DK = 256
DV = 512
SPAN = 64
SEQ = ("seq_0", "seq_1", "seq_2")


def nothing_yet(shard, identity):
    return jax.tree.map(
        lambda part, zero: jnp.zeros_like(part) + jnp.asarray(zero, part.dtype), shard, identity
    )


def prefix_by_axis(shard, axes, combine, identity):
    before = start = nothing_yet(shard, identity)
    subtotal = shard
    for axis in reversed(axes):
        length, position = (lax.axis_size(axis), lax.axis_index(axis))
        pieces = jax.tree.map(
            lambda part, kind: lax.all_gather(part.astype(kind), axis),
            subtotal,
            (jnp.bfloat16, jnp.bfloat16),
        )
        inside, subtotal = (start, start)
        for k in range(length):
            passed = k < position
            subtotal = combine(
                subtotal, jax.tree.map(lambda part, own: part[k].astype(own.dtype), pieces, shard)
            )
            inside = jax.tree.map(lambda new, old: jnp.where(passed, new, old), subtotal, inside)
        before = combine(inside, before)
    return before


def cut_along(shard, dim, length):
    before, after = (shard.shape[:dim], shard.shape[dim + 1 :])
    return jnp.moveaxis(shard.reshape(*before, length, -1, *after), dim, 0)


def summed_on_arrival(shard, axis, dim):
    length = lax.axis_size(axis)
    parts = lax.all_to_all(cut_along(shard, dim, length), axis, 0, 0, tiled=True)
    return jnp.sum(parts.astype(jnp.float32), axis=0)


def join_states(earlier, latter):
    return (earlier[0] + latter[0], jnp.exp(latter[0])[..., None, :] * earlier[1] + latter[1])


def shards(queries, key_vectors, values, log_gate, out_gate, norm_gain, out_weight):
    length = queries.shape[0]
    head_count = queries.shape[1] // DK
    blocks = length // SPAN
    middle_pos = SPAN // 2
    running = jnp.cumsum(log_gate.astype(jnp.float32).reshape(blocks, SPAN, head_count, DK), axis=1)
    middle = running[:, middle_pos : middle_pos + 1]
    ending = running[:, SPAN - 1 : SPAN]
    query_f = queries.reshape(blocks, SPAN, head_count, DK).astype(jnp.float32)
    key_f = key_vectors.reshape(blocks, SPAN, head_count, DK).astype(jnp.float32)
    q_inter = (query_f * jnp.exp(running)).astype(jnp.bfloat16)
    q_intra = (query_f * jnp.exp(running - middle)).astype(jnp.bfloat16)
    k_intra = (key_f * jnp.exp(middle - running)).astype(jnp.bfloat16)
    k_state = (key_f * jnp.exp(ending - running)).astype(jnp.bfloat16)
    value_blocks = values.reshape(blocks, SPAN, head_count, DV)
    block_state = jnp.einsum(
        "bthe,bthd->bhed", value_blocks, k_state, preferred_element_type=jnp.float32
    )
    block_log = ending[:, 0]
    run_log, run_state = lax.associative_scan(join_states, (block_log, block_state), axis=0)
    device_log = run_log[-1]
    device_state = run_state[-1]
    before_log = run_log - block_log
    before_state = jnp.concatenate([jnp.zeros_like(run_state[:1]), run_state[:-1]], axis=0)
    scores = jnp.einsum("bthd,bshd->bhts", q_intra, k_intra, preferred_element_type=jnp.float32)
    causal = lax.iota(jnp.int32, SPAN)[:, None] >= lax.iota(jnp.int32, SPAN)[None, :]
    weights = jnp.where(causal, scores, 0.0).astype(jnp.bfloat16)
    local_part = jnp.einsum(
        "bhts,bshe->bthe", weights, value_blocks, preferred_element_type=jnp.float32
    )
    zero_log = jnp.zeros_like(device_log)
    zero_state = jnp.zeros_like(device_state)
    incoming_log, incoming = prefix_by_axis(
        (device_log, device_state), SEQ, join_states, (zero_log, zero_state)
    )
    carried = jnp.exp(before_log)[..., None, :] * incoming[None] + before_state
    carried_low = carried.astype(jnp.bfloat16)
    carried_part = jnp.einsum(
        "bthd,bhed->bthe", q_inter, carried_low, preferred_element_type=jnp.float32
    )
    attention = local_part + carried_part
    spread = jnp.mean(attention * attention, axis=-1, keepdims=True)
    normed = attention * lax.rsqrt(spread + 1e-05) * norm_gain.reshape(head_count, DV)
    outer_f = out_gate.reshape(blocks, SPAN, head_count, DV).astype(jnp.float32)
    gated_out = (normed * jax.nn.silu(outer_f)).astype(jnp.bfloat16)
    partial_value = jnp.dot(
        gated_out.reshape(length, head_count * DV), out_weight, preferred_element_type=jnp.float32
    )
    return summed_on_arrival(partial_value.astype(jnp.bfloat16), "head", 1).astype(jnp.bfloat16)


def solution(mesh):
    split = Mesh(
        mesh.devices.reshape(4, 8, 2, mesh.shape["head"]), ("seq_0", "seq_1", "seq_2", "head")
    )
    in_specs = (
        P(SEQ, "head"),
        P(SEQ, "head"),
        P(SEQ, "head"),
        P(SEQ, "head"),
        P(SEQ, "head"),
        P("head"),
        P("head", None),
    )
    out_specs = P(SEQ, "head")
    return jax.shard_map(
        shards, mesh=split, in_specs=in_specs, out_specs=out_specs, check_vma=False
    )
```

profile of v0, /device:TPU:24, one launch (start us, length us, event | category | flops | bytes accessed | tf_op | source)
XLA Modules:
  0.0 163.6 jit_solution(14921206279857943041)
XLA Ops:
  8.4 1.8 %all_gather.24 = bf16[2,1,256]{2,1,0:T(2,128)(2,1)S(1)} all-gather(bf16[1,1,256]{2,1,0:T(2,128)(2,1)S(1)} %fusion.54), channel_id=1, replica_groups=mesh['seq_0'=4,'seq_1'=8,'seq_2'=2,'head'=4] {'seq_2'}, dimensions={0}, use_global_device_ids=true | all-gather | bytes 1536 | tf_op jit(solution)/shard_map/all_gather | solution.py:25
  10.3 1.5 fusion.29
  12.9 1.7 %copy-done.1 = f32[8,256,512]{2,1,0:T(8,128)} copy-done((f32[8,256,512]{2,1,0:T(8,128)}, f32[8,256,512]{2,1,0:T(8,128)S(1)}, u32[]{:S(2)}) %copy-start.1) | copy-done | bytes 4194328
  16.2 3.5 %pad.47 = f32[4,1,512,256]{2,3,0,1:T(8,128)} pad(f32[2,1,512,256]{2,3,0,1:T(8,128)} %pad_maximum_fusion.1, f32[]{:T(128)} %constant.18.clone.1), padding=0_1_1x0_0_0x0_0_0x0_0_0 | pad | bytes 3145732 | tf_op jit(solution)/shard_map/pad | solution.py:74
  19.7 2.4 %pad.48 = f32[4,1,512,256]{2,3,0,1:T(8,128)} pad(f32[2,1,512,256]{2,3,0,1:T(8,128)S(1)} %pad_add_fusion, f32[]{:T(128)} %constant.18.clone.1), padding=1_0_1x0_0_0x0_0_0x0_0_0 | pad | bytes 3145732 | tf_op jit(solution)/shard_map/pad | solution.py:74
  22.0 4.0 %add.317 = f32[4,1,512,256]{2,3,0,1:T(8,128)} add(f32[4,1,512,256]{2,3,0,1:T(8,128)} %pad.47, f32[4,1,512,256]{2,3,0,1:T(8,128)} %pad.48) | non-fusion elementwise | flops 524288 | bytes 6291456 | tf_op jit(solution)/shard_map/add | solution.py:74
  26.1 5.7 %pad.93 = f32[8,1,512,256]{2,3,0,1:T(8,128)} pad(f32[4,1,512,256]{2,3,0,1:T(8,128)} %add.317, f32[]{:T(128)} %constant.18.clone.1), padding=1_0_1x0_0_0x0_0_0x0_0_0 | pad | bytes 6291460
  31.8 2.6 %fusion.5 = f32[3,1,512,256]{2,3,0,1:T(8,128)S(1)} fusion(f32[4,1,512,256]{2,3,0,1:T(8,128)} %pad.48, f32[4,1,512,256]{2,3,0,1:T(8,128)} %pad.47, f32[8,1,512,256]{2,3,0,1:T(8,128)} %bitcast.111, f32[3,256]{1,0:T(4,128)S(1)} %get-tuple-element.34), kind=kLoop, calls=%fused_computation.10 | loop fusion | flops 1179648 | bytes 6294528 | tf_op jit(solution)/shard_map/add | solution.py:52
  35.5 1.5 pad_maximum_fusion
  37.0 5.8 %pad.49 = f32[8,1,512,256]{2,3,0,1:T(8,128)} pad(f32[4,1,512,256]{2,3,0,1:T(8,128)} %pad_maximum_fusion, f32[]{:T(128)} %constant.18.clone.1), padding=0_1_1x0_0_0x0_0_0x0_0_0 | pad | bytes 6291460 | tf_op jit(solution)/shard_map/pad | solution.py:74
  42.8 1.3 add_convert_fusion.1
  44.2 2.2 %all_gather.27 = bf16[2,1,512,256]{3,2,1,0:T(8,128)(2,1)S(1)} all-gather(bf16[1,1,512,256]{3,2,1,0:T(8,128)(2,1)S(1)} %copy.28), channel_id=1, replica_groups=mesh['seq_0'=4,'seq_1'=8,'seq_2'=2,'head'=4] {'seq_2'}, dimensions={0}, use_global_device_ids=true | all-gather | bytes 786432 | tf_op jit(solution)/shard_map/all_gather | solution.py:25
  47.2 19.2 %all_gather.25 = bf16[8,1,256]{2,1,0:T(2,128)(2,1)S(1)} all-gather(bf16[1,1,256]{2,1,0:T(2,128)(2,1)S(1)} %get-tuple-element.41), channel_id=1, replica_groups=mesh['seq_0'=4,'seq_1'=8,'seq_2'=2,'head'=4] {'seq_1'}, dimensions={0}, use_global_device_ids=true | all-gather | bytes 4608 | tf_op jit(solution)/shard_map/all_gather | solution.py:25
  66.4 24.4 %all-gather.3.cloned.1.call-done = bf16[8,1,512,256]{3,2,1,0:T(8,128)(2,1)} async-done(((bf16[1,1,512,256]{3,2,1,0:T(8,128)(2,1)}), bf16[8,1,512,256]{3,2,1,0:T(8,128)(2,1)}) %all-gather.3.cloned.1.call-update) | async-done | bytes 2097168 | tf_op jit(solution)/shard_map/all_gather | solution.py:25
  90.9 2.6 %fusion.34 = bf16[1,1,512,256]{3,2,1,0:T(8,128)(2,1)} fusion(f32[256]{0:T(256)S(1)} %bitcast.140, f32[256]{0:T(256)S(1)} %bitcast.128, f32[256]{0:T(256)S(1)} %bitcast.126, f32[256]{0:T(256)S(1)} %bitcast.138, f32[256]{0:T(256)S(1)} %bitcast.136, f32[256]{0:T(256)S(1)} %bitcast.134, f32[256]{0:T(256)S(1)} %bitcast.132, f32[256]{0:T(256)S(1)} %bitcast.130, ...), kind=kLoop, calls=%fused_computation.54 | loop fusion | flops 3145728 | bytes 2367488 | tf_op jit(solution)/shard_map/convert_element_type | solution.py:25
  93.6 5.6 %pad.61 = f32[7,1,512,256]{2,3,0,1:T(8,128)} pad(f32[4,1,512,256]{2,3,0,1:T(8,128)} %pad_maximum_fusion, f32[]{:T(128)} %constant.18.clone.1), padding=0_0_1x0_0_0x0_0_0x0_0_0 | pad | bytes 5767172 | tf_op jit(solution)/shard_map/slice | solution.py:78
  99.2 9.7 %all_gather.26 = bf16[4,1,256]{2,1,0:T(2,128)(2,1)S(1)} all-gather(bf16[1,1,256]{2,1,0:T(2,128)(2,1)S(1)} %get-tuple-element.20), channel_id=1, replica_groups=mesh['seq_0'=4,'seq_1'=8,'seq_2'=2,'head'=4] {'seq_0'}, dimensions={0}, use_global_device_ids=true | all-gather | bytes 2560 | tf_op jit(solution)/shard_map/all_gather | solution.py:25
  109.6 2.4 %convolution_bitcast_fusion = f32[8,512,64]{1,2,0:T(8,128)} fusion(bf16[8,64,512]{2,1,0:T(8,128)(2,1)S(1)} %bitcast.116, bf16[8,64,256]{2,0,1:T(8,128)(2,1)} %get-tuple-element.14, bf16[8,64,256]{2,0,1:T(8,128)(2,1)} %get-tuple-element.15, pred[64,64]{1,0:T(8,128)(4,1)S(1)} %iota_compare_fusion), kind=kOutput, calls=%fused_computation.13 | convolution fusion | flops 50397184 | bytes 2101248 | tf_op jit(solution)/shard_map/bhts,bshe->bthe/dot_general | solution.py:82
  112.1 5.9 %slice_add_fusion.4 = f32[7,1,512,256]{2,3,0,1:T(8,128)} fusion(f32[7,1,512,256]{2,3,0,1:T(8,128)} %pad.61, f32[8,1,512,256]{2,3,0,1:T(8,128)} %pad.93), kind=kLoop, calls=%fused_computation.153 | loop fusion | flops 917504 | bytes 11010048 | tf_op jit(solution)/shard_map/add | solution.py:74
  118.9 2.8 %add_bitcast_fusion = f32[512,256]{1,0:T(8,128)S(1)} fusion(bf16[4,1,512,256]{3,2,1,0:T(8,128)(2,1)} %all-gather.5.cloned.1.call-done, f32[256]{0:T(256)S(1)} %bitcast.145, f32[256]{0:T(256)S(1)} %bitcast.125, f32[256]{0:T(256)S(1)} %bitcast.123, f32[256]{0:T(256)S(1)} %bitcast.141, f32[256]{0:T(256)S(1)} %bitcast.129, f32[256]{0:T(256)S(1)} %bitcast.127, ...), kind=kLoop, calls=%fused_computation.52 | loop fusion | flops 7471104 | bytes 4210702 | tf_op jit(solution)/shard_map/mul | solution.py:90
  121.9 3.2 %multiply_reduce_fusion = (f32[8,64]{1,0:T(8,128)S(1)}, f32[8,1,512,64]{2,3,0,1:T(8,128)S(1)}) fusion(f32[8,512,64]{1,2,0:T(8,128)} %convolution_bitcast_fusion, f32[7,1,512,256]{2,3,0,1:T(8,128)} %slice_add_fusion.4, f32[512,256]{0,1:T(8,128)S(1)} %copy.29, f32[8,256]{1,0:T(8,128)S(1)} %exponential_bitcast_fusion, ...), kind=kOutput, calls=%fused_computation.26 | convolution fusion | flops 138149376 | bytes 6563840 | tf_op jit(solution)/shard_map/bthd,bhed->bthe/dot_general | solution.py:92
  125.5 1.3 convolution_convert_fusion
  127.0 26.9 %all_to_all.5 = bf16[4,512,512]{2,1,0:T(8,128)(2,1)} all-to-all(bf16[4,512,512]{2,1,0:T(8,128)(2,1)S(1)} %bitcast.113), channel_id=1, replica_groups=mesh['seq_0'=4,'seq_1'=8,'seq_2'=2,'head'=4] {'head'}, dimensions={0} | all-to-all | bytes 4194304 | tf_op jit(solution)/shard_map/all_to_all | solution.py:47
  153.9 2.9 %reduce_sum.22 = bf16[512,512]{1,0:T(8,128)(2,1)} reduce(bf16[4,512,512]{2,1,0:T(8,128)(2,1)} %all_to_all.5, bf16[]{:T(256)} %constant.48.clone.1), dimensions={0}, to_apply=%region_2.3 | reduce | flops 786432 | bytes 2621442 | tf_op jit(solution)/shard_map/reduce_sum | solution.py:48
  (68 shorter events, 9.1 us)
Async XLA Ops:
  6.5 119.0 %copy-start = (bf16[512,2048]{1,0:T(8,128)(2,1)S(1)}, bf16[512,2048]{1,0:T(8,128)(2,1)}, u32[]{:S(2)}) copy-start(bf16[512,2048]{1,0:T(8,128)(2,1)} %param.13) | copy-start | bytes 6291460
  6.5 3.7 %copy-start.6 = (bf16[512,256]{1,0:T(8,128)(2,1)S(1)}, bf16[512,256]{1,0:T(8,128)(2,1)}, u32[]{:S(2)}) copy-start(bf16[512,256]{1,0:T(8,128)(2,1)} %param.8) | copy-start | bytes 786436
  6.5 3.7 %copy-start.7 = (bf16[512,256]{1,0:T(8,128)(2,1)S(1)}, bf16[512,256]{1,0:T(8,128)(2,1)}, u32[]{:S(2)}) copy-start(bf16[512,256]{1,0:T(8,128)(2,1)} %param.7) | copy-start | bytes 786436
  6.5 84.3 %all-gather.3.cloned.1.call-start = ((), (), s32[]{:S(2)}) async-start(), calls=%async_computation.1 | async-start | bytes 2359296 | tf_op jit(solution)/shard_map/all_gather | solution.py:25
  8.1 3.8 %copy-start.2 = (f32[8,64,1,256]{3,0,1,2:T(8,128)}, f32[8,64,1,256]{3,0,1,2:T(8,128)S(1)}, u32[]{:S(2)}) copy-start(f32[8,64,1,256]{3,0,1,2:T(8,128)S(1)} %fusion.32) | copy-start | bytes 1572868
  10.2 1.7 %copy-start.3 = (bf16[512,512]{1,0:T(8,128)(2,1)S(1)}, bf16[512,512]{1,0:T(8,128)(2,1)}, u32[]{:S(2)}) copy-start(bf16[512,512]{1,0:T(8,128)(2,1)} %param.9) | copy-start | bytes 1572868
  12.6 2.0 %copy-start.1 = (f32[8,256,512]{2,1,0:T(8,128)}, f32[8,256,512]{2,1,0:T(8,128)S(1)}, u32[]{:S(2)}) copy-start(f32[8,256,512]{2,1,0:T(8,128)S(1)} %fusion.37) | copy-start | bytes 12582916
  47.2 71.7 %all-gather.5.cloned.1.call-start = ((), (), s32[]{:S(2)}) async-start(), calls=%async_computation.2 | async-start | bytes 1310720 | tf_op jit(solution)/shard_map/all_gather | solution.py:25
  93.6 16.1 %copy-start.4 = (bf16[512,512]{1,0:T(8,128)(2,1)S(1)}, bf16[512,512]{1,0:T(8,128)(2,1)}, u32[]{:S(2)}) copy-start(bf16[512,512]{1,0:T(8,128)(2,1)} %param.9) | copy-start | bytes 1572868
  121.9 3.2 %copy-start.5 = (bf16[512,512]{1,0:T(8,128)(2,1)S(1)}, bf16[512,512]{1,0:T(8,128)(2,1)}, u32[]{:S(2)}) copy-start(bf16[512,512]{1,0:T(8,128)(2,1)} %param.11) | copy-start | bytes 1572868
  121.9 3.2 %copy-start.8 = (f32[512]{0:T(512)S(1)}, f32[512]{0:T(512)}, u32[]{:S(2)}) copy-start(f32[512]{0:T(512)} %param.12) | copy-start | bytes 6148
Sparse Core Ops, SparseCore 0:
  47.3 43.5 all-gather.2
  93.7 25.1 all-gather.4
where the time goes:
time: 166 us; the launch traced here: 164 us
  blocking collectives  59.7 us (36%)
  other arithmetic  30.5 us (18%)
  local copies, waits for them, and re-layouts  26.4 us (16%)
  waiting for transfers between devices  25.4 us (15%)
  between operations  13.7 us (8%)
  matrix products  7.64 us (5%)
    all_gather x4, blocking collectives, prefix_by_axis(): lax.all_gather(part.astype(kind), axis)  32.9 us
    all_to_all x1, blocking collectives, summed_on_arrival(): lax.all_to_all(cut_along(shard, dim, length), axis, 0, 0, tiled=True)  26.9 us
    all_gather x2, waiting for transfers between devices, prefix_by_axis(): lax.all_gather(part.astype(kind), axis)  25.4 us
    pad x7, local copies, waits for them, and re-layouts, shards(): lax.associative_scan(join_states, (block_log, block_state), axis=0)  11.7 us
    add x5, other arithmetic, shards(): lax.associative_scan(join_states, (block_log, block_state), axis=0)  9.99 us
    unnamed x19, local copies, waits for them, and re-layouts  7.46 us
    slice x1, local copies, waits for them, and re-layouts, shards(): run_state[:-1]  5.59 us
    mul x2, other arithmetic, shards(): carried = jnp.exp(before_log)[..., None, :] * incoming[None] + before_state  3.52 us
  transfers between devices with their start and end apart: 2, of which 2 were waited for; matrix products, arithmetic and copies ran while one was open for 9% of the time, Pallas kernels for 0%

commit v1 on v0

v1 whole, which is shorter than its diff:
```python
import functools

import jax
import jax.numpy as jnp
from jax import lax
from jax.experimental import pallas as pl
from jax.experimental.pallas import tpu as pltpu
from jax.sharding import Mesh
from jax.sharding import PartitionSpec as P

DK = 256
DV = 512
SPAN = 64
LANE = 128
SEQ = ("seq_0", "seq_1", "seq_2")
F32 = jnp.float32
BF16 = jnp.bfloat16
VMEM = pl.BlockSpec(memory_space=pltpu.VMEM)


def call(body, outs, *args, flops=10**9):
    moved = sum(a.size * a.dtype.itemsize for a in args)
    return pl.pallas_call(
        body,
        out_shape=outs,
        in_specs=[VMEM] * len(args),
        out_specs=jax.tree.map(lambda _: VMEM, outs),
        cost_estimate=pl.CostEstimate(flops=flops, transcendentals=0, bytes_accessed=moved),
    )(*args)


def dot(a, b, dims=((1,), (0,))):
    return lax.dot_general(a, b, (dims, ((), ())), preferred_element_type=F32)


def triangle(length, keep):
    row = lax.broadcasted_iota(jnp.int32, (length, length), 0)
    col = lax.broadcasted_iota(jnp.int32, (length, length), 1)
    return jnp.where(keep(row, col), 1.0, 0.0).astype(BF16)


def state_body(k_ref, v_ref, g_ref, out_ref):
    length = k_ref.shape[0]
    pieces = out_ref.shape[0]
    gate = g_ref[...]
    after = dot(triangle(length, lambda r, c: c > r), gate)
    k_state = (k_ref[...].astype(F32) * jnp.exp(after)).astype(BF16)
    state = dot(v_ref[...], k_state, ((0,), (0,)))
    total = after[0:1] + gate[0:1].astype(F32)
    high = total.astype(BF16).astype(F32)
    low = total - high
    rows = state.shape[0] // pieces
    row = lax.broadcasted_iota(jnp.int32, (8, LANE), 0)
    tail = jnp.zeros((8, LANE), F32)
    for at, part in enumerate((high[:, :LANE], high[:, LANE:], low[:, :LANE], low[:, LANE:])):
        tail = jnp.where(row == at, part, tail)
    out_ref[:, 0:rows, :] = state[:, :LANE].reshape(pieces, rows, LANE).astype(BF16)
    out_ref[:, rows : 2 * rows, :] = state[:, LANE:].reshape(pieces, rows, LANE).astype(BF16)
    out_ref[:, 2 * rows :, :] = jnp.broadcast_to(tail[None], (pieces, 8, LANE)).astype(BF16)


def scan_body(in_ref, out_ref):
    pieces, rows = (in_ref.shape[0], out_ref.shape[1] // 2)
    left = right = jnp.zeros((rows, LANE), F32)
    for j in range(pieces):
        out_ref[j, 0:rows, :] = left.astype(BF16)
        out_ref[j, rows : 2 * rows, :] = right.astype(BF16)
        tail = in_ref[j, 2 * rows :, :].astype(F32)
        left = left * jnp.exp(tail[0:1] + tail[2:3]) + in_ref[j, 0:rows, :].astype(F32)
        right = right * jnp.exp(tail[1:2] + tail[3:4]) + in_ref[j, rows : 2 * rows, :].astype(F32)


def local_body(q_ref, k_ref, v_ref, g_ref, att_ref, q_out_ref):
    length = q_ref.shape[0]
    lower = triangle(SPAN, lambda r, c: c <= r)
    row = lax.broadcasted_iota(jnp.int32, (SPAN, SPAN), 0)
    col = lax.broadcasted_iota(jnp.int32, (SPAN, SPAN), 1)
    carried = None
    before = jnp.zeros((1, DK), F32)
    for i in range(length // SPAN):
        at = slice(i * SPAN, (i + 1) * SPAN)
        running = dot(lower, g_ref[at, :])
        middle = running[SPAN // 2 : SPAN // 2 + 1]
        ending = running[SPAN - 1 : SPAN]
        query_f = q_ref[at, :].astype(F32)
        key_f = k_ref[at, :].astype(F32)
        value = v_ref[at, :]
        q_inter = query_f * jnp.exp(running)
        q_intra = (query_f * jnp.exp(running - middle)).astype(BF16)
        k_intra = (key_f * jnp.exp(middle - running)).astype(BF16)
        scores = dot(q_intra, k_intra, ((1,), (1,)))
        weights = jnp.where(col <= row, scores, 0.0).astype(BF16)
        attention = dot(weights, value)
        if i:
            attention = attention + dot(q_inter.astype(BF16), carried.astype(BF16))
        att_ref[at, :] = attention
        q_out_ref[at, :] = (query_f * jnp.exp(running + before)).astype(BF16)
        before = before + ending
        if (i + 1) * SPAN < length:
            k_state = (key_f * jnp.exp(ending - running)).T.astype(BF16)
            block = dot(k_state, value)
            carried = block if i == 0 else carried * jnp.exp(ending).reshape(DK, 1) + block


def finish_body(s_ref, q_ref, att_ref, outer_ref, gain_ref, w_ref, gated_ref, far_ref):
    pieces, rows = (s_ref.shape[0], s_ref.shape[1] // 2)
    count = lax.axis_size("head")
    far = lax.rem(lax.axis_index("head") + count // 2, count)
    s_left = s_ref[:, 0:rows, :].reshape(pieces * rows, LANE)
    s_right = s_ref[:, rows : 2 * rows, :].reshape(pieces * rows, LANE)
    attention = att_ref[...]
    attention = attention + dot(q_ref[:, :LANE], s_left, ((1,), (1,)))
    attention = attention + dot(q_ref[:, LANE:], s_right, ((1,), (1,)))
    spread = jnp.mean(attention * attention, axis=-1, keepdims=True)
    normed = attention * lax.rsqrt(spread + 1e-05) * gain_ref[...]
    outer_f = outer_ref[...].astype(F32)
    gated = (normed * (outer_f / (1.0 + jnp.exp(-outer_f)))).astype(BF16)
    gated_ref[...] = gated
    width = far_ref.shape[1]
    start = pl.multiple_of(far * width, width)
    far_ref[...] = dot(gated, w_ref[:, pl.ds(start, width)]).astype(BF16)


def near_body(gated_ref, w_ref, up_ref, down_ref, own_ref):
    count = lax.axis_size("head")
    me = lax.axis_index("head")
    width = own_ref.shape[1]
    gated = gated_ref[...]
    for ref, shift in ((up_ref, 1), (down_ref, count - 1), (own_ref, 0)):
        start = pl.multiple_of(lax.rem(me + shift, count) * width, width)
        ref[...] = dot(gated, w_ref[:, pl.ds(start, width)]).astype(BF16)


def ring(axis, shift):
    length = lax.axis_size(axis)
    return [(i, (i + shift) % length) for i in range(length)]


def shards(queries, key_vectors, values, log_gate, out_gate, norm_gain, out_weight):
    length = queries.shape[0]
    pieces = lax.axis_size(SEQ)
    rows = DV // pieces
    shape = jax.ShapeDtypeStruct
    sent = call(
        state_body,
        shape((pieces, 2 * rows + 8, LANE), BF16),
        key_vectors,
        values,
        log_gate,
    )
    slices = lax.all_to_all(sent, SEQ, 0, 0, tiled=True)
    att_local, q_start = call(
        local_body,
        (shape((length, DV), F32), shape((length, DK), BF16)),
        queries,
        key_vectors,
        values,
        log_gate,
    )
    prefixes = call(scan_body, shape((pieces, 2 * rows, LANE), BF16), slices)
    incoming = lax.all_to_all(prefixes, SEQ, 0, 0, tiled=True)
    width = out_weight.shape[1] // lax.axis_size("head")
    block = shape((length, width), BF16)
    gated, far = call(
        finish_body,
        (shape((length, DV), BF16), block),
        incoming,
        q_start,
        att_local,
        out_gate,
        norm_gain.reshape(1, DV),
        out_weight,
    )
    half = length // 2
    far_up = lax.ppermute(far[:half], "head", ring("head", 1))
    far_down = lax.ppermute(far[half:], "head", ring("head", -1))
    up, down, own = call(near_body, (block, block, block), gated, out_weight)
    up_a = (up[:half].astype(F32) + far_up.astype(F32)).astype(BF16)
    down_b = (down[half:].astype(F32) + far_down.astype(F32)).astype(BF16)
    from_down_b = lax.ppermute(up[half:], "head", ring("head", 1))
    from_up_a = lax.ppermute(down[:half], "head", ring("head", -1))
    from_down_a = lax.ppermute(up_a, "head", ring("head", 1))
    from_up_b = lax.ppermute(down_b, "head", ring("head", -1))
    out_a = own[:half].astype(F32) + from_up_a.astype(F32) + from_down_a.astype(F32)
    out_b = own[half:].astype(F32) + from_up_b.astype(F32) + from_down_b.astype(F32)
    return jnp.concatenate([out_a, out_b], axis=0).astype(BF16)


def solution(mesh):
    split = Mesh(
        mesh.devices.reshape(4, 8, 2, mesh.shape["head"]), ("seq_0", "seq_1", "seq_2", "head")
    )
    in_specs = (
        P(SEQ, "head"),
        P(SEQ, "head"),
        P(SEQ, "head"),
        P(SEQ, "head"),
        P(SEQ, "head"),
        P("head"),
        P("head", None),
    )
    out_specs = P(SEQ, "head")
    return jax.shard_map(
        shards, mesh=split, in_specs=in_specs, out_specs=out_specs, check_vma=False
    )
```

time: 166 us -> 80.3 us (0.48); the launches traced: 164 us -> 79.8 us
  blocking collectives: 59.7 us -> 26.5 us
  other arithmetic: 30.5 us -> 2.24 us
  local copies, waits for them, and re-layouts: 26.4 us -> 4.56 us
  Pallas kernels: 0 us -> 17.6 us
  between operations: 13.7 us -> 0.06 us
  starting transfers between devices: 0.04 us -> 13.3 us
  waiting for transfers between devices: 25.4 us -> 15.5 us
  matrix products: 7.64 us -> 0 us
    all_gather x4 -> x0, blocking collectives: 32.9 us -> none  [prefix_by_axis(): lax.all_gather(part.astype(kind), axis)]
    all_gather x2 -> x0, waiting for transfers between devices: 25.4 us -> none  [prefix_by_axis(): lax.all_gather(part.astype(kind), axis)]
    pallas_call x0 -> x5, Pallas kernels: none -> 17.6 us  [call(): pl.pallas_call(body, out_shape=outs, in_specs=[VMEM] * len(args), out_spe...]
    add x12 -> x0, other arithmetic: 13.2 us -> none  [the longest x5 9.99 us: shards(): lax.associative_scan(join_states, (block_log, block_state), axis=0)]
    pad x7 -> x0, local copies, waits for them, and re-layouts: 11.7 us -> none  [shards(): lax.associative_scan(join_states, (block_log, block_state), axis=0)]
    ppermute x0 -> x6, waiting for transfers between devices: none -> 8.93 us  [the longest x1 2.51 us: shards(): from_up_b = lax.ppermute(down_b, 'head', ring('head', -1))]
    dot_general x4 -> x0, matrix products: 7.64 us -> none  [the longest x1 3.19 us: shards(): jnp.einsum('bthd,bhed->bthe', q_inter, carried_low, preferred_element_typ...]
    ppermute x0 -> x6, starting transfers between devices: none -> 7.02 us  [the longest x1 2.73 us: shards(): from_down_a = lax.ppermute(up_a, 'head', ring('head', 1))]
  transfers between devices with their start and end apart: 2 -> 7, of which waited for: 2 -> 5; matrix products, arithmetic and copies ran while one was open for 9% -> 5% of each run, Pallas kernels for 0% -> 11%
where the time goes in v1:
time: 80.3 us; the launch traced here: 79.8 us
  blocking collectives  26.5 us (33%)
  Pallas kernels  17.6 us (22%)
  waiting for transfers between devices  15.5 us (19%)
  starting transfers between devices  13.3 us (17%)
  local copies, waits for them, and re-layouts  4.56 us (6%)
  other arithmetic  2.24 us (3%)
    all_to_all x1, blocking collectives, shards(): slices = lax.all_to_all(sent, SEQ, 0, 0, tiled=True)  26.5 us
    pallas_call x5, Pallas kernels, call(): pl.pallas_call(body, out_shape=outs, in_specs=[VMEM] * len(args), out_spe...  17.6 us
    all_to_all x1, waiting for transfers between devices, shards(): incoming = lax.all_to_all(prefixes, SEQ, 0, 0, tiled=True)  6.58 us
    all_to_all x1, starting transfers between devices, shards(): incoming = lax.all_to_all(prefixes, SEQ, 0, 0, tiled=True)  6.3 us
    ppermute x1, starting transfers between devices, shards(): from_down_a = lax.ppermute(up_a, 'head', ring('head', 1))  2.73 us
    ppermute x1, waiting for transfers between devices, shards(): from_up_b = lax.ppermute(down_b, 'head', ring('head', -1))  2.51 us
    ppermute x1, waiting for transfers between devices, shards(): from_down_a = lax.ppermute(up_a, 'head', ring('head', 1))  2.36 us
    ppermute x1, waiting for transfers between devices, shards(): from_down_b = lax.ppermute(up[half:], 'head', ring('head', 1))  2.27 us
  transfers between devices with their start and end apart: 7, of which 5 were waited for; matrix products, arithmetic and copies ran while one was open for 5% of the time, Pallas kernels for 11%

profile of v1, /device:TPU:24, one launch (start us, length us, event | category | flops | bytes accessed | tf_op | source)
XLA Modules:
  0.0 79.8 jit_solution(492186529462615379)
XLA Ops:
  0.0 2.7 %shard_map.73 = bf16[64,24,128]{2,1,0:T(8,128)(2,1)} custom-call(bf16[512,256]{1,0:T(8,128)(2,1)} %k_ref.3, bf16[512,512]{1,0:T(8,128)(2,1)} %v_ref.3, bf16[512,256]{1,0:T(8,128)(2,1)} %g_ref.3), custom_call_target="tpu_custom_call" | custom-call | flops 1000000000 | bytes 1048576 | tf_op jit(solution)/shard_map/pallas_call | solution.py:23
  2.7 26.5 %all_to_all.10.in_ref = bf16[64,24,128]{2,1,0:T(8,128)(2,1)} all-to-all(bf16[64,24,128]{2,1,0:T(8,128)(2,1)} %shard_map.73), channel_id=1, replica_groups=mesh['seq_0'=4,'seq_1'=8,'seq_2'=2,'head'=4] {'seq_0','seq_1','seq_2'}, dimensions={0} | all-to-all | bytes 786432 | tf_op jit(solution)/shard_map/all_to_all | solution.py:151
  29.2 1.8 %shard_map.74 = bf16[64,16,128]{2,1,0:T(8,128)(2,1)} custom-call(bf16[64,24,128]{2,1,0:T(8,128)(2,1)} %all_to_all.10.in_ref), custom_call_target="tpu_custom_call" | custom-call | flops 1000000000 | bytes 393216 | tf_op jit(solution)/shard_map/pallas_call | solution.py:23
  31.1 6.3 %all-to-all-start.1 = ((bf16[64,16,128]{2,1,0:T(8,128)(2,1)}), bf16[64,16,128]{2,1,0:T(8,128)(2,1)S(1)}, u32[]{:S(2)}, u32[]{:S(2)}) async-start(bf16[64,16,128]{2,1,0:T(8,128)(2,1)} %shard_map.74), calls=%async_computation.1 | async-start | bytes 524288 | tf_op jit(solution)/shard_map/all_to_all | solution.py:161
  37.4 5.4 %shard_map.75 = (f32[512,512]{1,0:T(8,128)}, bf16[512,256]{1,0:T(8,128)(2,1)}) custom-call(bf16[512,256]{1,0:T(8,128)(2,1)} %q_ref.1, bf16[512,256]{1,0:T(8,128)(2,1)} %k_ref.3, bf16[512,512]{1,0:T(8,128)(2,1)} %v_ref.3, bf16[512,256]{1,0:T(8,128)(2,1)} %g_ref.3), custom_call_target="tpu_custom_call" | custom-call | flops 1000000000 | bytes 1310720 | tf_op jit(solution)/shard_map/pallas_call | solution.py:23
  42.8 6.6 %all-to-all-done.1.s_ref = bf16[64,16,128]{2,1,0:T(8,128)(2,1)S(1)} async-done(((bf16[64,16,128]{2,1,0:T(8,128)(2,1)}), bf16[64,16,128]{2,1,0:T(8,128)(2,1)S(1)}, u32[]{:S(2)}, u32[]{:S(2)}) %all-to-all-start.1) | async-done | bytes 262176 | tf_op jit(solution)/shard_map/all_to_all | solution.py:161
  49.3 0.7 copy-done
  50.0 4.1 %shard_map.76 = (bf16[512,512]{1,0:T(8,128)(2,1)}, bf16[512,512]{1,0:T(8,128)(2,1)}) custom-call(bf16[64,16,128]{2,1,0:T(8,128)(2,1)} %copy-done, bf16[512,256]{1,0:T(8,128)(2,1)} %get-tuple-element.12.q_ref, f32[512,512]{1,0:T(8,128)} %get-tuple-element.13.att_ref, bf16[512,512]{1,0:T(8,128)(2,1)} %outer_ref.1, f32[1,512]{1,0:T(1,128)} %bitcast.1, ...), custom_call_target="tpu_custom_call" | custom-call | flops 1000000000 | bytes 4196352 | tf_op jit(solution)/shard_map/pallas_call | solution.py:23
  54.2 1.1 %fusion = (bf16[256,512]{1,0:T(8,128)(2,1)S(1)}, bf16[256,512]{1,0:T(8,128)(2,1)S(1)}) fusion(bf16[512,512]{1,0:T(8,128)(2,1)} %get-tuple-element.18), kind=kLoop, calls=%fused_computation.5 | loop fusion | bytes 1048576 | tf_op jit(solution)/shard_map/slice | solution.py:175
  55.2 0.3 collective-permute-start.1
  55.5 1.8 %collective-permute-start.3 = (bf16[256,512]{1,0:T(8,128)(2,1)S(1)}, bf16[256,512]{1,0:T(8,128)(2,1)S(1)}, u32[]{:S(2)}, u32[]{:S(2)}) collective-permute-start(bf16[256,512]{1,0:T(8,128)(2,1)S(1)} %get-tuple-element.22), channel_id=1, source_target_pairs={{0,3},{1,0},{2,1},{3,2},{4,7},{5,4},{6,5},{7,6},{8,11},{9,8},{10,9... | collective-permute-start | bytes 786440 | tf_op jit(solution)/shard_map/ppermute | solution.py:176
  57.3 3.6 %shard_map.77 = (bf16[512,512]{1,0:T(8,128)(2,1)}, bf16[512,512]{1,0:T(8,128)(2,1)}, bf16[512,512]{1,0:T(8,128)(2,1)}) custom-call(bf16[512,512]{1,0:T(8,128)(2,1)} %get-tuple-element.14.gated_ref, bf16[512,2048]{1,0:T(8,128)(2,1)} %w_ref.3), custom_call_target="tpu_custom_call" | custom-call | flops 1000000000 | bytes 2621440 | tf_op jit(solution)/shard_map/pallas_call | solution.py:23
  60.9 1.0 %slice.25 = bf16[256,512]{1,0:T(8,128)(2,1)S(1)} slice(bf16[512,512]{1,0:T(8,128)(2,1)} %get-tuple-element.16), slice={[0:256], [0:512]} | slice | bytes 524288 | tf_op jit(solution)/shard_map/slice | solution.py:181
  62.0 1.0 %slice.31 = bf16[256,512]{1,0:T(8,128)(2,1)S(1)} slice(bf16[512,512]{1,0:T(8,128)(2,1)} %get-tuple-element.17), slice={[256:512], [0:512]} | slice | bytes 524288 | tf_op jit(solution)/shard_map/slice | solution.py:180
  62.9 1.5 %collective-permute-start.5 = (bf16[256,512]{1,0:T(8,128)(2,1)S(1)}, bf16[256,512]{1,0:T(8,128)(2,1)S(1)}, u32[]{:S(2)}, u32[]{:S(2)}) collective-permute-start(bf16[256,512]{1,0:T(8,128)(2,1)S(1)} %slice.31), channel_id=1, source_target_pairs={{0,1},{1,2},{2,3},{3,0},{4,5},{5,6},{6,7},{7,4},{8,9},{9,10},{10,1... | collective-permute-start | bytes 786440 | tf_op jit(solution)/shard_map/ppermute | solution.py:180
  64.5 0.6 collective-permute-start
  65.0 1.0 %add_convert_fusion.3 = bf16[256,512]{1,0:T(8,128)(2,1)S(1)} fusion(bf16[256,512]{1,0:T(8,128)(2,1)S(1)} %collective-permute-done.1, bf16[512,512]{1,0:T(8,128)(2,1)} %get-tuple-element.17), kind=kLoop, calls=%fused_computation.4 | loop fusion | flops 524288 | bytes 786432 | tf_op jit(solution)/shard_map/convert_element_type | solution.py:178
  66.1 2.7 %collective-permute-start.2 = (bf16[256,512]{1,0:T(8,128)(2,1)S(1)}, bf16[256,512]{1,0:T(8,128)(2,1)S(1)}, u32[]{:S(2)}, u32[]{:S(2)}) collective-permute-start(bf16[256,512]{1,0:T(8,128)(2,1)S(1)} %add_convert_fusion.3), channel_id=1, source_target_pairs={{0,1},{1,2},{2,3},{3,0},{4,5},{5,6},{6,7},{7,4},{8,9},{9,10},{10,1... | collective-permute-start | bytes 786440 | tf_op jit(solution)/shard_map/ppermute | solution.py:182
  68.8 1.0 %add_convert_fusion.1 = bf16[256,512]{1,0:T(8,128)(2,1)S(1)} fusion(bf16[256,512]{1,0:T(8,128)(2,1)S(1)} %collective-permute-done.3, bf16[512,512]{1,0:T(8,128)(2,1)} %get-tuple-element.16), kind=kLoop, calls=%fused_computation.2 | loop fusion | flops 524288 | bytes 786432 | tf_op jit(solution)/shard_map/convert_element_type | solution.py:179
  69.9 2.3 %collective-permute-done.5 = bf16[256,512]{1,0:T(8,128)(2,1)S(1)} collective-permute-done((bf16[256,512]{1,0:T(8,128)(2,1)S(1)}, bf16[256,512]{1,0:T(8,128)(2,1)S(1)}, u32[]{:S(2)}, u32[]{:S(2)}) %collective-permute-start.5) | collective-permute-done | bytes 262176 | tf_op jit(solution)/shard_map/ppermute | solution.py:180
  72.2 1.8 %collective-permute-done = bf16[256,512]{1,0:T(8,128)(2,1)S(1)} collective-permute-done((bf16[256,512]{1,0:T(8,128)(2,1)S(1)}, bf16[256,512]{1,0:T(8,128)(2,1)S(1)}, u32[]{:S(2)}, u32[]{:S(2)}) %collective-permute-start) | collective-permute-done | bytes 262176 | tf_op jit(solution)/shard_map/ppermute | solution.py:181
  74.0 2.4 %collective-permute-done.2 = bf16[256,512]{1,0:T(8,128)(2,1)S(1)} collective-permute-done((bf16[256,512]{1,0:T(8,128)(2,1)S(1)}, bf16[256,512]{1,0:T(8,128)(2,1)S(1)}, u32[]{:S(2)}, u32[]{:S(2)}) %collective-permute-start.2) | collective-permute-done | bytes 262176 | tf_op jit(solution)/shard_map/ppermute | solution.py:182
  76.3 2.5 %collective-permute-done.4 = bf16[256,512]{1,0:T(8,128)(2,1)S(1)} collective-permute-done((bf16[256,512]{1,0:T(8,128)(2,1)S(1)}, bf16[256,512]{1,0:T(8,128)(2,1)S(1)}, u32[]{:S(2)}, u32[]{:S(2)}) %collective-permute-start.4) | collective-permute-done | bytes 262176 | tf_op jit(solution)/shard_map/ppermute | solution.py:183
  79.1 0.8 copy-done.2
  (9 shorter events, 0.3 us)
Async XLA Ops:
  31.1 18.3 %all-to-all-start.1 = ((bf16[64,16,128]{2,1,0:T(8,128)(2,1)}), bf16[64,16,128]{2,1,0:T(8,128)(2,1)S(1)}, u32[]{:S(2)}, u32[]{:S(2)}) async-start(bf16[64,16,128]{2,1,0:T(8,128)(2,1)} %shard_map.74), calls=%async_computation.1 | async-start | bytes 524288 | tf_op jit(solution)/shard_map/all_to_all | solution.py:161
  49.3 0.7 copy-start
  55.2 9.8 %collective-permute-start.1 = (bf16[256,512]{1,0:T(8,128)(2,1)S(1)}, bf16[256,512]{1,0:T(8,128)(2,1)S(1)}, u32[]{:S(2)}, u32[]{:S(2)}) collective-permute-start(bf16[256,512]{1,0:T(8,128)(2,1)S(1)} %get-tuple-element.21), channel_id=1, source_target_pairs={{0,1},{1,2},{2,3},{3,0},{4,5},{5,6},{6,7},{7,4},{8,9},{9,10},{10,1... | collective-permute-start | bytes 786440 | tf_op jit(solution)/shard_map/ppermute | solution.py:175
  55.5 13.2 %collective-permute-start.3 = (bf16[256,512]{1,0:T(8,128)(2,1)S(1)}, bf16[256,512]{1,0:T(8,128)(2,1)S(1)}, u32[]{:S(2)}, u32[]{:S(2)}) collective-permute-start(bf16[256,512]{1,0:T(8,128)(2,1)S(1)} %get-tuple-element.22), channel_id=1, source_target_pairs={{0,3},{1,0},{2,1},{3,2},{4,7},{5,4},{6,5},{7,6},{8,11},{9,8},{10,9... | collective-permute-start | bytes 786440 | tf_op jit(solution)/shard_map/ppermute | solution.py:176
  60.9 17.9 %copy-start.1 = (bf16[512,512]{1,0:T(8,128)(2,1)S(1)}, bf16[512,512]{1,0:T(8,128)(2,1)}, u32[]{:S(2)}) copy-start(bf16[512,512]{1,0:T(8,128)(2,1)} %get-tuple-element.15) | copy-start | bytes 1572868
  62.9 9.3 %collective-permute-start.5 = (bf16[256,512]{1,0:T(8,128)(2,1)S(1)}, bf16[256,512]{1,0:T(8,128)(2,1)S(1)}, u32[]{:S(2)}, u32[]{:S(2)}) collective-permute-start(bf16[256,512]{1,0:T(8,128)(2,1)S(1)} %slice.31), channel_id=1, source_target_pairs={{0,1},{1,2},{2,3},{3,0},{4,5},{5,6},{6,7},{7,4},{8,9},{9,10},{10,1... | collective-permute-start | bytes 786440 | tf_op jit(solution)/shard_map/ppermute | solution.py:180
  64.5 9.5 %collective-permute-start = (bf16[256,512]{1,0:T(8,128)(2,1)S(1)}, bf16[256,512]{1,0:T(8,128)(2,1)S(1)}, u32[]{:S(2)}, u32[]{:S(2)}) collective-permute-start(bf16[256,512]{1,0:T(8,128)(2,1)S(1)} %slice.25), channel_id=1, source_target_pairs={{0,3},{1,0},{2,1},{3,2},{4,7},{5,4},{6,5},{7,6},{8,11},{9,8},{10,9... | collective-permute-start | bytes 786440 | tf_op jit(solution)/shard_map/ppermute | solution.py:181
  66.1 10.3 %collective-permute-start.2 = (bf16[256,512]{1,0:T(8,128)(2,1)S(1)}, bf16[256,512]{1,0:T(8,128)(2,1)S(1)}, u32[]{:S(2)}, u32[]{:S(2)}) collective-permute-start(bf16[256,512]{1,0:T(8,128)(2,1)S(1)} %add_convert_fusion.3), channel_id=1, source_target_pairs={{0,1},{1,2},{2,3},{3,0},{4,5},{5,6},{6,7},{7,4},{8,9},{9,10},{10,1... | collective-permute-start | bytes 786440 | tf_op jit(solution)/shard_map/ppermute | solution.py:182
  69.8 9.0 %collective-permute-start.4 = (bf16[256,512]{1,0:T(8,128)(2,1)S(1)}, bf16[256,512]{1,0:T(8,128)(2,1)S(1)}, u32[]{:S(2)}, u32[]{:S(2)}) collective-permute-start(bf16[256,512]{1,0:T(8,128)(2,1)S(1)} %add_convert_fusion.1), channel_id=1, source_target_pairs={{0,3},{1,0},{2,1},{3,2},{4,7},{5,4},{6,5},{7,6},{8,11},{9,8},{10,9... | collective-permute-start | bytes 786440 | tf_op jit(solution)/shard_map/ppermute | solution.py:183
  79.0 0.8 copy-start.2

commit v2 on v1

--- a/solution.py
+++ b/solution.py
@@ -26,6 +26,7 @@
         in_specs=[VMEM] * len(args),
         out_specs=jax.tree.map(lambda _: VMEM, outs),
         cost_estimate=pl.CostEstimate(flops=flops, transcendentals=0, bytes_accessed=moved),
+        compiler_params=pltpu.CompilerParams(vmem_limit_bytes=16 * 2**20),
     )(*args)
 
 

time: 80.3 us -> 74.8 us (0.932)
  Pallas kernels: 17.6 us -> 6.69 us
  local copies, waits for them, and re-layouts: 4.56 us -> 10.4 us
  waiting for transfers between devices: 15.5 us -> 17.5 us
  other arithmetic: 2.24 us -> 0.33 us
    pallas_call x5, Pallas kernels: 17.6 us -> 6.69 us  [call(): pl.pallas_call(body, out_shape=outs, in_specs=[VMEM] * len(args), out_spe...]
    unnamed x6 -> x26, local copies, waits for them, and re-layouts: 1.5 us -> 10.3 us
    ppermute x1, waiting for transfers between devices: 0.01 us -> 4 us  [shards(): far_up = lax.ppermute(far[:half], 'head', ring('head', 1))]
    all_to_all x1, waiting for transfers between devices: 6.58 us -> 4.22 us  [shards(): incoming = lax.all_to_all(prefixes, SEQ, 0, 0, tiled=True)]
    ppermute x1, starting transfers between devices: 2.73 us -> 1.51 us  [shards(): from_down_a = lax.ppermute(up_a, 'head', ring('head', 1))]
    ppermute x1, waiting for transfers between devices: 2.51 us -> 1.3 us  [shards(): from_up_b = lax.ppermute(down_b, 'head', ring('head', -1))]
    slice x1, local copies, waits for them, and re-layouts: 1.06 us -> 0.04 us  [shards(): far_up = lax.ppermute(far[:half], 'head', ring('head', 1))]
    ppermute x1, waiting for transfers between devices: 2.27 us -> 3.29 us  [shards(): from_down_b = lax.ppermute(up[half:], 'head', ring('head', 1))]
  transfers between devices with their start and end apart: 7 -> 7, of which waited for: 5 -> 6; matrix products, arithmetic and copies ran while one was open for 5% -> 0% of each run, Pallas kernels for 11% -> 6%
where the time goes in v2:
time: 74.8 us; the launch traced here: 74.1 us
  blocking collectives  26.2 us (35%)
  waiting for transfers between devices  17.5 us (23%)
  starting transfers between devices  12.8 us (17%)
  local copies, waits for them, and re-layouts  10.4 us (14%)
  Pallas kernels  6.69 us (9%)
    all_to_all x1, blocking collectives, shards(): slices = lax.all_to_all(sent, SEQ, 0, 0, tiled=True)  26.2 us
    unnamed x26, local copies, waits for them, and re-layouts  10.3 us
    pallas_call x5, Pallas kernels, call(): pl.pallas_call(body, out_shape=outs, in_specs=[VMEM] * len(args), out_spe...  6.69 us
    all_to_all x1, starting transfers between devices, shards(): incoming = lax.all_to_all(prefixes, SEQ, 0, 0, tiled=True)  6.43 us
    all_to_all x1, waiting for transfers between devices, shards(): incoming = lax.all_to_all(prefixes, SEQ, 0, 0, tiled=True)  4.22 us
    ppermute x1, waiting for transfers between devices, shards(): far_up = lax.ppermute(far[:half], 'head', ring('head', 1))  4 us
    ppermute x1, waiting for transfers between devices, shards(): from_down_b = lax.ppermute(up[half:], 'head', ring('head', 1))  3.29 us
    ppermute x1, waiting for transfers between devices, shards(): from_down_a = lax.ppermute(up_a, 'head', ring('head', 1))  3.27 us
  transfers between devices with their start and end apart: 7, of which 6 were waited for; matrix products, arithmetic and copies ran while one was open for 0% of the time, Pallas kernels for 6%

profile of v2, /device:TPU:24, one launch (start us, length us, event | category | flops | bytes accessed | tf_op | source)
XLA Modules:
  0.0 74.1 jit_solution(8368298329349421762)
XLA Ops:
  0.0 1.0 %copy-done.5 = bf16[512,512]{1,0:T(8,128)(2,1)S(1)} copy-done((bf16[512,512]{1,0:T(8,128)(2,1)S(1)}, bf16[512,512]{1,0:T(8,128)(2,1)}, u32[]{:S(2)}) %copy-start.5) | copy-done | bytes 524312
  1.0 0.9 %copy-done.7 = bf16[512,256]{1,0:T(8,128)(2,1)S(1)} copy-done((bf16[512,256]{1,0:T(8,128)(2,1)S(1)}, bf16[512,256]{1,0:T(8,128)(2,1)}, u32[]{:S(2)}) %copy-start.7) | copy-done | bytes 262168
  2.0 0.9 %copy-done.9 = bf16[512,256]{1,0:T(8,128)(2,1)S(1)} copy-done((bf16[512,256]{1,0:T(8,128)(2,1)S(1)}, bf16[512,256]{1,0:T(8,128)(2,1)}, u32[]{:S(2)}) %copy-start.9) | copy-done | bytes 262168
  3.7 26.2 %all_to_all.10.in_ref = bf16[64,24,128]{2,1,0:T(8,128)(2,1)S(1)} all-to-all(bf16[64,24,128]{2,1,0:T(8,128)(2,1)S(1)} %shard_map.73), channel_id=1, replica_groups=mesh['seq_0'=4,'seq_1'=8,'seq_2'=2,'head'=4] {'seq_0','seq_1','seq_2'}, dimensions={0} | all-to-all | bytes 786432 | tf_op jit(solution)/shard_map/all_to_all | solution.py:152
  29.9 0.8 %shard_map.74 = bf16[64,16,128]{2,1,0:T(8,128)(2,1)} custom-call(bf16[64,24,128]{2,1,0:T(8,128)(2,1)S(1)} %all_to_all.10.in_ref), custom_call_target="tpu_custom_call" | custom-call | flops 1000000000 | bytes 393216 | tf_op jit(solution)/shard_map/pallas_call | solution.py:23
  30.8 6.4 %all-to-all-start.1 = ((bf16[64,16,128]{2,1,0:T(8,128)(2,1)}), bf16[64,16,128]{2,1,0:T(8,128)(2,1)S(1)}, u32[]{:S(2)}, u32[]{:S(2)}) async-start(bf16[64,16,128]{2,1,0:T(8,128)(2,1)} %shard_map.74), calls=%async_computation.1 | async-start | bytes 524288 | tf_op jit(solution)/shard_map/all_to_all | solution.py:162
  37.2 1.0 %copy-done.6 = bf16[512,512]{1,0:T(8,128)(2,1)S(1)} copy-done((bf16[512,512]{1,0:T(8,128)(2,1)S(1)}, bf16[512,512]{1,0:T(8,128)(2,1)}, u32[]{:S(2)}) %copy-start.6) | copy-done | bytes 524312
  38.3 0.9 %copy-done.8 = bf16[512,256]{1,0:T(8,128)(2,1)S(1)} copy-done((bf16[512,256]{1,0:T(8,128)(2,1)S(1)}, bf16[512,256]{1,0:T(8,128)(2,1)}, u32[]{:S(2)}) %copy-start.8) | copy-done | bytes 262168
  39.2 0.9 %copy-done.10 = bf16[512,256]{1,0:T(8,128)(2,1)S(1)} copy-done((bf16[512,256]{1,0:T(8,128)(2,1)S(1)}, bf16[512,256]{1,0:T(8,128)(2,1)}, u32[]{:S(2)}) %copy-start.10) | copy-done | bytes 262168
  40.2 0.9 %copy-done.11 = bf16[512,256]{1,0:T(8,128)(2,1)S(1)} copy-done((bf16[512,256]{1,0:T(8,128)(2,1)S(1)}, bf16[512,256]{1,0:T(8,128)(2,1)}, u32[]{:S(2)}) %copy-start.11) | copy-done | bytes 262168
  41.1 3.1 %shard_map.75 = (f32[512,512]{1,0:T(8,128)S(1)}, bf16[512,256]{1,0:T(8,128)(2,1)S(1)}) custom-call(bf16[512,256]{1,0:T(8,128)(2,1)S(1)} %copy-done.11, bf16[512,256]{1,0:T(8,128)(2,1)S(1)} %copy-done.8, bf16[512,512]{1,0:T(8,128)(2,1)S(1)} %copy-done.6, bf16[512,256]{1,0:T(8,128)(2,1)S(1)} %copy-done.10), custom_call_target="tpu_custom_call" | custom-call | flops 1000000000 | bytes 1310720 | tf_op jit(solution)/shard_map/pallas_call | solution.py:23
  45.0 4.2 %all-to-all-done.1.s_ref = bf16[64,16,128]{2,1,0:T(8,128)(2,1)S(1)} async-done(((bf16[64,16,128]{2,1,0:T(8,128)(2,1)}), bf16[64,16,128]{2,1,0:T(8,128)(2,1)S(1)}, u32[]{:S(2)}, u32[]{:S(2)}) %all-to-all-start.1) | async-done | bytes 262176 | tf_op jit(solution)/shard_map/all_to_all | solution.py:162
  49.2 1.0 %copy-done.1 = bf16[512,512]{1,0:T(8,128)(2,1)S(1)} copy-done((bf16[512,512]{1,0:T(8,128)(2,1)S(1)}, bf16[512,512]{1,0:T(8,128)(2,1)}, u32[]{:S(2)}) %copy-start.1) | copy-done | bytes 524312
  50.2 0.9 %copy-done.3 = bf16[512,256]{1,0:T(8,128)(2,1)S(1)} copy-done((bf16[512,256]{1,0:T(8,128)(2,1)S(1)}, bf16[512,256]{1,0:T(8,128)(2,1)}, u32[]{:S(2)}) %copy-start.3) | copy-done | bytes 262168
  51.2 1.0 %shard_map.76 = (bf16[512,512]{1,0:T(8,128)(2,1)S(1)}, bf16[512,512]{1,0:T(8,128)(2,1)S(1)}) custom-call(bf16[64,16,128]{2,1,0:T(8,128)(2,1)S(1)} %all-to-all-done.1.s_ref, bf16[512,256]{1,0:T(8,128)(2,1)S(1)} %copy-done.3, f32[512,512]{1,0:T(8,128)S(1)} %get-tuple-element.13.att_ref, bf16[512,512]{1,0:T(8,128)(2,1)S(1)} %copy-done.1, f32[1,512]{1,0:T(1,128)S(1)} %bitcast.1, ...), custom_call_target="tpu_custom_call" | custom-call | flops 1000000000 | bytes 4196352 | tf_op jit(solution)/shard_map/pallas_call | solution.py:23
  52.5 1.8 %collective-permute-start.3 = (bf16[256,512]{1,0:T(8,128)(2,1)S(1)}, bf16[256,512]{1,0:T(8,128)(2,1)S(1)}, u32[]{:S(2)}, u32[]{:S(2)}) collective-permute-start(bf16[256,512]{1,0:T(8,128)(2,1)S(1)} %get-tuple-element.22), channel_id=1, source_target_pairs={{0,3},{1,0},{2,1},{3,2},{4,7},{5,4},{6,5},{7,6},{8,11},{9,8},{10,9... | collective-permute-start | bytes 786440 | tf_op jit(solution)/shard_map/ppermute | solution.py:177
  54.3 1.0 %shard_map.77 = (bf16[512,512]{1,0:T(8,128)(2,1)S(1)}, bf16[512,512]{1,0:T(8,128)(2,1)S(1)}, bf16[512,512]{1,0:T(8,128)(2,1)S(1)}) custom-call(bf16[512,512]{1,0:T(8,128)(2,1)S(1)} %get-tuple-element.14.gated_ref, bf16[512,2048]{1,0:T(8,128)(2,1)S(1)} %copy-done), custom_call_target="tpu_custom_call" | custom-call | flops 1000000000 | bytes 2621440 | tf_op jit(solution)/shard_map/pallas_call | solution.py:23
  55.4 1.5 %collective-permute-start.5 = (bf16[256,512]{1,0:T(8,128)(2,1)S(1)}, bf16[256,512]{1,0:T(8,128)(2,1)S(1)}, u32[]{:S(2)}, u32[]{:S(2)}) collective-permute-start(bf16[256,512]{1,0:T(8,128)(2,1)S(1)} %slice.31), channel_id=1, source_target_pairs={{0,1},{1,2},{2,3},{3,0},{4,5},{5,6},{6,7},{7,4},{8,9},{9,10},{10,1... | collective-permute-start | bytes 786440 | tf_op jit(solution)/shard_map/ppermute | solution.py:181
  57.5 4.0 %collective-permute-done.1 = bf16[256,512]{1,0:T(8,128)(2,1)S(1)} collective-permute-done((bf16[256,512]{1,0:T(8,128)(2,1)S(1)}, bf16[256,512]{1,0:T(8,128)(2,1)S(1)}, u32[]{:S(2)}, u32[]{:S(2)}) %collective-permute-start.1) | collective-permute-done | bytes 262176 | tf_op jit(solution)/shard_map/ppermute | solution.py:176
  61.5 1.5 %collective-permute-start.2 = (bf16[256,512]{1,0:T(8,128)(2,1)S(1)}, bf16[256,512]{1,0:T(8,128)(2,1)S(1)}, u32[]{:S(2)}, u32[]{:S(2)}) collective-permute-start(bf16[256,512]{1,0:T(8,128)(2,1)S(1)} %add_convert_fusion.3), channel_id=1, source_target_pairs={{0,1},{1,2},{2,3},{3,0},{4,5},{5,6},{6,7},{7,4},{8,9},{9,10},{10,1... | collective-permute-start | bytes 786440 | tf_op jit(solution)/shard_map/ppermute | solution.py:183
  63.8 3.3 %collective-permute-done.5 = bf16[256,512]{1,0:T(8,128)(2,1)S(1)} collective-permute-done((bf16[256,512]{1,0:T(8,128)(2,1)S(1)}, bf16[256,512]{1,0:T(8,128)(2,1)S(1)}, u32[]{:S(2)}, u32[]{:S(2)}) %collective-permute-start.5) | collective-permute-done | bytes 262176 | tf_op jit(solution)/shard_map/ppermute | solution.py:181
  67.1 1.4 %collective-permute-done = bf16[256,512]{1,0:T(8,128)(2,1)S(1)} collective-permute-done((bf16[256,512]{1,0:T(8,128)(2,1)S(1)}, bf16[256,512]{1,0:T(8,128)(2,1)S(1)}, u32[]{:S(2)}, u32[]{:S(2)}) %collective-permute-start) | collective-permute-done | bytes 262176 | tf_op jit(solution)/shard_map/ppermute | solution.py:182
  68.5 3.3 %collective-permute-done.2 = bf16[256,512]{1,0:T(8,128)(2,1)S(1)} collective-permute-done((bf16[256,512]{1,0:T(8,128)(2,1)S(1)}, bf16[256,512]{1,0:T(8,128)(2,1)S(1)}, u32[]{:S(2)}, u32[]{:S(2)}) %collective-permute-start.2) | collective-permute-done | bytes 262176 | tf_op jit(solution)/shard_map/ppermute | solution.py:183
  71.8 1.3 %collective-permute-done.4 = bf16[256,512]{1,0:T(8,128)(2,1)S(1)} collective-permute-done((bf16[256,512]{1,0:T(8,128)(2,1)S(1)}, bf16[256,512]{1,0:T(8,128)(2,1)S(1)}, u32[]{:S(2)}, u32[]{:S(2)}) %collective-permute-start.4) | collective-permute-done | bytes 262176 | tf_op jit(solution)/shard_map/ppermute | solution.py:184
  (29 shorter events, 4.2 us)
Async XLA Ops:
  0.0 1.0 %copy-start.5 = (bf16[512,512]{1,0:T(8,128)(2,1)S(1)}, bf16[512,512]{1,0:T(8,128)(2,1)}, u32[]{:S(2)}) copy-start(bf16[512,512]{1,0:T(8,128)(2,1)} %v_ref.3) | copy-start | bytes 1572868
  1.0 0.9 %copy-start.7 = (bf16[512,256]{1,0:T(8,128)(2,1)S(1)}, bf16[512,256]{1,0:T(8,128)(2,1)}, u32[]{:S(2)}) copy-start(bf16[512,256]{1,0:T(8,128)(2,1)} %k_ref.3) | copy-start | bytes 786436
  2.0 0.9 %copy-start.9 = (bf16[512,256]{1,0:T(8,128)(2,1)S(1)}, bf16[512,256]{1,0:T(8,128)(2,1)}, u32[]{:S(2)}) copy-start(bf16[512,256]{1,0:T(8,128)(2,1)} %g_ref.3) | copy-start | bytes 786436
  30.8 18.4 %copy-start = (bf16[512,2048]{1,0:T(8,128)(2,1)S(1)}, bf16[512,2048]{1,0:T(8,128)(2,1)}, u32[]{:S(2)}) copy-start(bf16[512,2048]{1,0:T(8,128)(2,1)} %w_ref.3) | copy-start | bytes 6291460
  30.8 18.4 %copy-start.4 = (f32[512]{0:T(512)S(1)}, f32[512]{0:T(512)}, u32[]{:S(2)}) copy-start(f32[512]{0:T(512)} %param.12) | copy-start | bytes 6148
  30.8 18.4 %all-to-all-start.1 = ((bf16[64,16,128]{2,1,0:T(8,128)(2,1)}), bf16[64,16,128]{2,1,0:T(8,128)(2,1)S(1)}, u32[]{:S(2)}, u32[]{:S(2)}) async-start(bf16[64,16,128]{2,1,0:T(8,128)(2,1)} %shard_map.74), calls=%async_computation.1 | async-start | bytes 524288 | tf_op jit(solution)/shard_map/all_to_all | solution.py:162
  37.2 1.0 %copy-start.6 = (bf16[512,512]{1,0:T(8,128)(2,1)S(1)}, bf16[512,512]{1,0:T(8,128)(2,1)}, u32[]{:S(2)}) copy-start(bf16[512,512]{1,0:T(8,128)(2,1)} %v_ref.3) | copy-start | bytes 1572868
  38.3 0.9 %copy-start.8 = (bf16[512,256]{1,0:T(8,128)(2,1)S(1)}, bf16[512,256]{1,0:T(8,128)(2,1)}, u32[]{:S(2)}) copy-start(bf16[512,256]{1,0:T(8,128)(2,1)} %k_ref.3) | copy-start | bytes 786436
  39.2 0.9 %copy-start.10 = (bf16[512,256]{1,0:T(8,128)(2,1)S(1)}, bf16[512,256]{1,0:T(8,128)(2,1)}, u32[]{:S(2)}) copy-start(bf16[512,256]{1,0:T(8,128)(2,1)} %g_ref.3) | copy-start | bytes 786436
  40.2 0.9 %copy-start.11 = (bf16[512,256]{1,0:T(8,128)(2,1)S(1)}, bf16[512,256]{1,0:T(8,128)(2,1)}, u32[]{:S(2)}) copy-start(bf16[512,256]{1,0:T(8,128)(2,1)} %q_ref.1) | copy-start | bytes 786436
  44.3 0.7 copy-start.2
  49.2 1.0 %copy-start.1 = (bf16[512,512]{1,0:T(8,128)(2,1)S(1)}, bf16[512,512]{1,0:T(8,128)(2,1)}, u32[]{:S(2)}) copy-start(bf16[512,512]{1,0:T(8,128)(2,1)} %outer_ref.1) | copy-start | bytes 1572868
  50.2 0.9 %copy-start.3 = (bf16[512,256]{1,0:T(8,128)(2,1)S(1)}, bf16[512,256]{1,0:T(8,128)(2,1)}, u32[]{:S(2)}) copy-start(bf16[512,256]{1,0:T(8,128)(2,1)} %copy-done.2) | copy-start | bytes 786436
  52.2 9.3 %collective-permute-start.1 = (bf16[256,512]{1,0:T(8,128)(2,1)S(1)}, bf16[256,512]{1,0:T(8,128)(2,1)S(1)}, u32[]{:S(2)}, u32[]{:S(2)}) collective-permute-start(bf16[256,512]{1,0:T(8,128)(2,1)S(1)} %get-tuple-element.21), channel_id=1, source_target_pairs={{0,1},{1,2},{2,3},{3,0},{4,5},{5,6},{6,7},{7,4},{8,9},{9,10},{10,1... | collective-permute-start | bytes 786440 | tf_op jit(solution)/shard_map/ppermute | solution.py:176
  52.5 10.5 %collective-permute-start.3 = (bf16[256,512]{1,0:T(8,128)(2,1)S(1)}, bf16[256,512]{1,0:T(8,128)(2,1)S(1)}, u32[]{:S(2)}, u32[]{:S(2)}) collective-permute-start(bf16[256,512]{1,0:T(8,128)(2,1)S(1)} %get-tuple-element.22), channel_id=1, source_target_pairs={{0,3},{1,0},{2,1},{3,2},{4,7},{5,4},{6,5},{7,6},{8,11},{9,8},{10,9... | collective-permute-start | bytes 786440 | tf_op jit(solution)/shard_map/ppermute | solution.py:177
  55.4 11.7 %collective-permute-start.5 = (bf16[256,512]{1,0:T(8,128)(2,1)S(1)}, bf16[256,512]{1,0:T(8,128)(2,1)S(1)}, u32[]{:S(2)}, u32[]{:S(2)}) collective-permute-start(bf16[256,512]{1,0:T(8,128)(2,1)S(1)} %slice.31), channel_id=1, source_target_pairs={{0,1},{1,2},{2,3},{3,0},{4,5},{5,6},{6,7},{7,4},{8,9},{9,10},{10,1... | collective-permute-start | bytes 786440 | tf_op jit(solution)/shard_map/ppermute | solution.py:181
  56.9 11.7 %collective-permute-start = (bf16[256,512]{1,0:T(8,128)(2,1)S(1)}, bf16[256,512]{1,0:T(8,128)(2,1)S(1)}, u32[]{:S(2)}, u32[]{:S(2)}) collective-permute-start(bf16[256,512]{1,0:T(8,128)(2,1)S(1)} %slice.25), channel_id=1, source_target_pairs={{0,3},{1,0},{2,1},{3,2},{4,7},{5,4},{6,5},{7,6},{8,11},{9,8},{10,9... | collective-permute-start | bytes 786440 | tf_op jit(solution)/shard_map/ppermute | solution.py:182
  61.5 10.2 %collective-permute-start.2 = (bf16[256,512]{1,0:T(8,128)(2,1)S(1)}, bf16[256,512]{1,0:T(8,128)(2,1)S(1)}, u32[]{:S(2)}, u32[]{:S(2)}) collective-permute-start(bf16[256,512]{1,0:T(8,128)(2,1)S(1)} %add_convert_fusion.3), channel_id=1, source_target_pairs={{0,1},{1,2},{2,3},{3,0},{4,5},{5,6},{6,7},{7,4},{8,9},{9,10},{10,1... | collective-permute-start | bytes 786440 | tf_op jit(solution)/shard_map/ppermute | solution.py:183
  63.1 10.0 %collective-permute-start.4 = (bf16[256,512]{1,0:T(8,128)(2,1)S(1)}, bf16[256,512]{1,0:T(8,128)(2,1)S(1)}, u32[]{:S(2)}, u32[]{:S(2)}) collective-permute-start(bf16[256,512]{1,0:T(8,128)(2,1)S(1)} %add_convert_fusion.1), channel_id=1, source_target_pairs={{0,3},{1,0},{2,1},{3,2},{4,7},{5,4},{6,5},{7,6},{8,11},{9,8},{10,9... | collective-permute-start | bytes 786440 | tf_op jit(solution)/shard_map/ppermute | solution.py:184
  73.3 0.8 %copy-start.12 = (bf16[512,512]{1,0:T(8,128)(2,1)}, bf16[512,512]{1,0:T(8,128)(2,1)S(1)}, u32[]{:S(2)}) copy-start(bf16[512,512]{1,0:T(8,128)(2,1)S(1)} %get-tuple-element.37) | copy-start | bytes 1572868

commit v3 on v2

v3 whole, which is shorter than its diff:
```python
import jax
import jax.numpy as jnp
from jax import lax
from jax.experimental import pallas as pl
from jax.experimental.pallas import tpu as pltpu
from jax.sharding import Mesh
from jax.sharding import PartitionSpec as P

DK = 256
DV = 512
SPAN = 64
LANE = 128
SEQ = ("chip_x", "chip_z", "core")
CHIPS = ("chip_x", "chip_z")
F32 = jnp.float32
BF16 = jnp.bfloat16
VMEM = pl.BlockSpec(memory_space=pltpu.VMEM)
HBM = pl.BlockSpec(memory_space=pltpu.HBM)


def call(body, outs, *args, fetched=(), flops=10**9):
    moved = sum(a.size * a.dtype.itemsize for a in args)
    scratch = [pltpu.VMEM(args[i].shape, args[i].dtype) for i in fetched]
    if fetched:
        scratch.append(pltpu.SemaphoreType.DMA((len(fetched),)))
    return pl.pallas_call(
        body,
        out_shape=outs,
        in_specs=[HBM if i in fetched else VMEM for i in range(len(args))],
        out_specs=jax.tree.map(lambda _: VMEM, outs),
        scratch_shapes=scratch,
        cost_estimate=pl.CostEstimate(flops=flops, transcendentals=0, bytes_accessed=moved),
        compiler_params=pltpu.CompilerParams(vmem_limit_bytes=16 * 2**20),
    )(*args)


def dot(a, b, dims=((1,), (0,))):
    return lax.dot_general(a, b, (dims, ((), ())), preferred_element_type=F32)


def triangle(length, keep):
    row = lax.broadcasted_iota(jnp.int32, (length, length), 0)
    col = lax.broadcasted_iota(jnp.int32, (length, length), 1)
    return jnp.where(keep(row, col), 1.0, 0.0).astype(BF16)


def stacked(*parts):
    row = lax.broadcasted_iota(jnp.int32, (8, LANE), 0)
    block = jnp.zeros((8, LANE), F32)
    for at, part in enumerate(parts):
        block = jnp.where(row == at, part, block)
    return block


def split_bf16(values):
    high = values.astype(BF16).astype(F32)
    return high, values - high


def state_body(k_hbm, v_hbm, g_hbm, own_ref, log_ref, swap_ref, k_ref, v_ref, g_ref, sems):
    copies = [
        pltpu.make_async_copy(src, dst, sems.at[i])
        for i, (src, dst) in enumerate(((g_hbm, g_ref), (k_hbm, k_ref), (v_hbm, v_ref)))
    ]
    for copy in copies:
        copy.start()
    length = k_ref.shape[0]
    half = DV // 2
    mask = triangle(length, lambda r, c: c > r)
    copies[0].wait()
    gate = g_ref[...]
    after = dot(mask, gate)
    total = after[0:1] + gate[0:1].astype(F32)
    copies[1].wait()
    k_state = (k_ref[...].astype(F32) * jnp.exp(after)).astype(BF16)
    copies[2].wait()
    core = lax.axis_index("core")
    theirs = pl.ds(pl.multiple_of((1 - core) * half, half), half)
    state = dot(v_ref[:, theirs], k_state, ((0,), (0,))).astype(BF16)
    swap_ref[0:half, :] = state[:, :LANE]
    swap_ref[half : 2 * half, :] = state[:, LANE:]
    left_high, left_low = split_bf16(total[:, :LANE])
    right_high, right_low = split_bf16(total[:, LANE:])
    tail = stacked(left_high, right_high, left_low, right_low)
    swap_ref[2 * half :, :] = jnp.concatenate([tail, tail], axis=0).astype(BF16)
    mine = pl.ds(pl.multiple_of(core * half, half), half)
    state = dot(v_ref[:, mine], k_state, ((0,), (0,)))
    own_ref[0:half, :] = state[:, :LANE]
    own_ref[half:, :] = state[:, LANE:]
    log_ref[...] = stacked(total[:, :LANE], total[:, LANE:])


def join_body(own_ref, log_ref, swap_ref, out_ref, first_ref, decay_ref):
    pieces, rows = (out_ref.shape[0], (out_ref.shape[1] - 8) // 2)
    half = pieces * rows
    early = lax.axis_index("core") == 0
    tail = swap_ref[2 * half : 2 * half + 8, :].astype(F32)
    sums = []
    decays = []
    for side in range(2):
        at = slice(side * half, (side + 1) * half)
        own_log = log_ref[side : side + 1, :]
        other_log = tail[side : side + 1] + tail[side + 2 : side + 3]
        own = own_ref[at, :]
        other = swap_ref[at, :].astype(F32)
        first = jnp.where(early, own, other)
        second = jnp.where(early, other, own)
        state = first * jnp.exp(jnp.where(early, other_log, own_log)) + second
        first_ref[at, :] = first
        decays.append(jnp.exp(jnp.where(early, own_log, other_log)))
        sums.append(own_log + other_log)
        piece = slice(side * rows, (side + 1) * rows)
        out_ref[:, piece, :] = state.reshape(pieces, rows, LANE).astype(BF16)
    decay_ref[...] = stacked(*decays)
    left_high, left_low = split_bf16(sums[0])
    right_high, right_low = split_bf16(sums[1])
    tail = stacked(left_high, right_high, left_low, right_low)
    out_ref[:, 2 * rows :, :] = jnp.broadcast_to(tail[None], (pieces, 8, LANE)).astype(BF16)


def scan_body(in_ref, out_ref):
    pieces, rows = (in_ref.shape[0], out_ref.shape[1] // 2)
    left = right = jnp.zeros((rows, LANE), F32)
    for j in range(pieces):
        out_ref[j, 0:rows, :] = left.astype(BF16)
        out_ref[j, rows : 2 * rows, :] = right.astype(BF16)
        tail = in_ref[j, 2 * rows :, :].astype(F32)
        left = left * jnp.exp(tail[0:1] + tail[2:3]) + in_ref[j, 0:rows, :].astype(F32)
        right = right * jnp.exp(tail[1:2] + tail[3:4]) + in_ref[j, rows : 2 * rows, :].astype(F32)


def part_body(in_ref, first_ref, decay_ref, keep_ref, send_ref):
    pieces, rows = (in_ref.shape[0], in_ref.shape[1] // 2)
    half = pieces * rows
    early = lax.axis_index("core") == 0
    for side in range(2):
        at = slice(side * half, (side + 1) * half)
        piece = slice(side * rows, (side + 1) * rows)
        entering = in_ref[:, piece, :].astype(F32).reshape(half, LANE)
        between = entering * decay_ref[side : side + 1, :] + first_ref[at, :]
        keep_ref[at, :] = jnp.where(early, entering, between).astype(BF16)
        send_ref[at, :] = jnp.where(early, between, entering).astype(BF16)


def local_body(
    q_hbm, k_hbm, v_hbm, g_hbm, outer_hbm, gain_ref, att_ref, start_ref, scale_ref,
    q_ref, k_ref, v_ref, g_ref, outer_ref, sems,
):
    pairs = ((g_hbm, g_ref), (q_hbm, q_ref), (k_hbm, k_ref), (v_hbm, v_ref), (outer_hbm, outer_ref))
    copies = [pltpu.make_async_copy(src, dst, sems.at[i]) for i, (src, dst) in enumerate(pairs)]
    for copy in copies:
        copy.start()
    length = q_ref.shape[0]
    lower = triangle(SPAN, lambda r, c: c <= r)
    row = lax.broadcasted_iota(jnp.int32, (SPAN, SPAN), 0)
    col = lax.broadcasted_iota(jnp.int32, (SPAN, SPAN), 1)
    for copy in copies:
        copy.wait()
    carried = None
    before = jnp.zeros((1, DK), F32)
    for i in range(length // SPAN):
        at = slice(i * SPAN, (i + 1) * SPAN)
        running = dot(lower, g_ref[at, :])
        middle = running[SPAN // 2 : SPAN // 2 + 1]
        ending = running[SPAN - 1 : SPAN]
        query_f = q_ref[at, :].astype(F32)
        key_f = k_ref[at, :].astype(F32)
        value = v_ref[at, :]
        q_inter = query_f * jnp.exp(running)
        q_intra = (query_f * jnp.exp(running - middle)).astype(BF16)
        k_intra = (key_f * jnp.exp(middle - running)).astype(BF16)
        scores = dot(q_intra, k_intra, ((1,), (1,)))
        weights = jnp.where(col <= row, scores, 0.0).astype(BF16)
        attention = dot(weights, value)
        if i:
            attention = attention + dot(q_inter.astype(BF16), carried.astype(BF16))
        att_ref[at, :] = attention
        start_ref[at, :] = (query_f * jnp.exp(running + before)).astype(BF16)
        before = before + ending
        if (i + 1) * SPAN < length:
            k_state = (key_f * jnp.exp(ending - running)).T.astype(BF16)
            block = dot(k_state, value)
            carried = block if i == 0 else carried * jnp.exp(ending).reshape(DK, 1) + block
        outer_f = outer_ref[at, :].astype(F32)
        scale_ref[at, :] = outer_f / (1.0 + jnp.exp(-outer_f)) * gain_ref[...]


def columns(index, width):
    return pl.ds(pl.multiple_of(index * width, width), width)


def finish_body(
    keep_ref, other_ref, q_ref, att_ref, scale_ref, w_hbm, gated_ref, far_a_ref, far_b_ref,
    w_ref, sems,
):
    count = lax.axis_size("head")
    width = far_a_ref.shape[1]
    far = lax.rem(lax.axis_index("head") + count // 2, count)
    copy = pltpu.make_async_copy(
        w_hbm.at[:, columns(far, width)], w_ref.at[:, columns(0, width)], sems.at[0]
    )
    copy.start()
    half = DV // 2
    core = lax.axis_index("core")
    total = 0.0
    parts = []
    for ref, place in ((keep_ref, core), (other_ref, 1 - core)):
        attention = att_ref[:, columns(place, half)]
        attention = attention + dot(q_ref[:, :LANE], ref[:half, :], ((1,), (1,)))
        attention = attention + dot(q_ref[:, LANE:], ref[half:, :], ((1,), (1,)))
        total = total + jnp.sum(attention * attention, axis=-1, keepdims=True)
        parts.append((attention, place))
    inverse = lax.rsqrt(total * (1.0 / DV) + 1e-05)
    for attention, place in parts:
        at = columns(place, half)
        gated_ref[:, at] = (attention * inverse * scale_ref[:, at]).astype(BF16)
    copy.wait()
    rows = far_a_ref.shape[0]
    weight = w_ref[:, 0:width]
    far_a_ref[...] = dot(gated_ref[:rows, :], weight).astype(BF16)
    far_b_ref[...] = dot(gated_ref[rows:, :], weight).astype(BF16)


def near_body(gated_ref, w_hbm, up_ref, down_ref, own_ref, w_ref, sems):
    count = lax.axis_size("head")
    width = own_ref.shape[1]
    me = lax.axis_index("head")
    copy = pltpu.make_async_copy(w_hbm, w_ref, sems.at[0])
    copy.start()
    copy.wait()
    for ref, shift in ((up_ref, 1), (down_ref, count - 1), (own_ref, 0)):
        ref[...] = dot(gated_ref[...], w_ref[:, columns(lax.rem(me + shift, count), width)])


def pass_body(up_ref, down_ref, far_up_ref, far_down_ref, up_out_ref, down_out_ref):
    rows = far_up_ref.shape[0]
    up_out_ref[:rows, :] = (up_ref[:rows, :] + far_up_ref[...].astype(F32)).astype(BF16)
    up_out_ref[rows:, :] = up_ref[rows:, :].astype(BF16)
    down_out_ref[:rows, :] = down_ref[:rows, :].astype(BF16)
    down_out_ref[rows:, :] = (down_ref[rows:, :] + far_down_ref[...].astype(F32)).astype(BF16)


def sum_body(own_ref, below_ref, above_ref, out_ref):
    total = own_ref[...] + below_ref[...].astype(F32) + above_ref[...].astype(F32)
    out_ref[...] = total.astype(BF16)


def ring(axis, shift):
    length = lax.axis_size(axis)
    return [(i, (i + shift) % length) for i in range(length)]


def shards(queries, key_vectors, values, log_gate, out_gate, norm_gain, out_weight):
    length = queries.shape[0]
    pieces = lax.axis_size(CHIPS)
    half = DV // 2
    rows = half // pieces
    shape = jax.ShapeDtypeStruct
    small = shape((8, LANE), F32)
    own, own_log, swap = call(
        state_body,
        (shape((DV, LANE), F32), small, shape((DV + 16, LANE), BF16)),
        key_vectors,
        values,
        log_gate,
        fetched=(0, 1, 2),
    )
    swapped = lax.ppermute(swap, "core", ring("core", 1))
    sent, first, decay = call(
        join_body,
        (shape((pieces, 2 * rows + 8, LANE), BF16), shape((DV, LANE), F32), small),
        own,
        own_log,
        swapped,
    )
    slices = lax.all_to_all(sent, CHIPS, 0, 0, tiled=True)
    att_local, q_start, scale = call(
        local_body,
        (shape((length, DV), F32), shape((length, DK), BF16), shape((length, DV), F32)),
        queries,
        key_vectors,
        values,
        log_gate,
        out_gate,
        norm_gain.reshape(1, DV),
        fetched=(0, 1, 2, 3, 4),
    )
    prefixes = call(scan_body, shape((pieces, 2 * rows, LANE), BF16), slices)
    entering = lax.all_to_all(prefixes, CHIPS, 0, 0, tiled=True)
    state_half = shape((DV, LANE), BF16)
    keep, send = call(part_body, (state_half, state_half), entering, first, decay)
    other = lax.ppermute(send, "core", ring("core", 1))
    width = out_weight.shape[1] // lax.axis_size("head")
    near = shape((length // 2, width), BF16)
    gated, far_a, far_b = call(
        finish_body,
        (shape((length, DV), BF16), near, near),
        keep,
        other,
        q_start,
        att_local,
        scale,
        out_weight,
        fetched=(5,),
    )
    far_up = lax.ppermute(far_a, "head", ring("head", 1))
    far_down = lax.ppermute(far_b, "head", ring("head", -1))
    block = shape((length, width), F32)
    up, down, own_part = call(near_body, (block, block, block), gated, out_weight, fetched=(1,))
    block = shape((length, width), BF16)
    to_up, to_down = call(pass_body, (block, block), up, down, far_up, far_down)
    below = lax.ppermute(to_up, "head", ring("head", 1))
    above = lax.ppermute(to_down, "head", ring("head", -1))
    return call(sum_body, block, own_part, below, above)


def solution(mesh):
    split = Mesh(mesh.devices.reshape(4, 8, 2, mesh.shape["head"]), (*SEQ, "head"))
    in_specs = (
        P(SEQ, "head"),
        P(SEQ, "head"),
        P(SEQ, "head"),
        P(SEQ, "head"),
        P(SEQ, "head"),
        P("head"),
        P("head", None),
    )
    out_specs = P(SEQ, "head")
    return jax.shard_map(
        shards, mesh=split, in_specs=in_specs, out_specs=out_specs, check_vma=False
    )
```

time: 74.8 us -> 74 us (0.989)
  blocking collectives: 26.2 us -> 37.3 us
  starting transfers between devices: 12.8 us -> 4.39 us
  local copies, waits for them, and re-layouts: 10.4 us -> 2.98 us
  waiting for transfers between devices: 17.5 us -> 20.7 us
  Pallas kernels: 6.69 us -> 8.19 us
    all_to_all x1 -> x2, blocking collectives: 26.2 us -> 37.3 us  [the longest x1 22.8 us: shards(): slices = lax.all_to_all(sent, CHIPS, 0, 0, tiled=True)]
    ppermute x6, waiting for transfers between devices: 13.3 us -> 20.7 us  [the longest x1 11.3 us: shards(): below = lax.ppermute(to_up, 'head', ring('head', 1))]
    unnamed x26 -> x20, local copies, waits for them, and re-layouts: 10.3 us -> 2.98 us
    all_to_all x1 -> x0, starting transfers between devices: 6.43 us -> none  [shards(): incoming = lax.all_to_all(prefixes, SEQ, 0, 0, tiled=True)]
    all_to_all x1 -> x0, waiting for transfers between devices: 4.22 us -> none  [shards(): incoming = lax.all_to_all(prefixes, SEQ, 0, 0, tiled=True)]
    ppermute x6, starting transfers between devices: 6.39 us -> 4.39 us  [the longest x1 1.81 us: shards(): far_down = lax.ppermute(far_b, 'head', ring('head', -1))]
    pallas_call x5 -> x9, Pallas kernels: 6.69 us -> 8.19 us  [call(): pl.pallas_call(body, out_shape=outs, in_specs=[HBM if i in fetched else V...]
  transfers between devices with their start and end apart: 7 -> 6, of which waited for: 6 -> 5; matrix products, arithmetic and copies ran while one was open for 0% -> 0% of each run, Pallas kernels for 6% -> 6%
where the time goes in v3:
time: 74 us; the launch traced here: 73.7 us
  blocking collectives  37.3 us (50%)
  waiting for transfers between devices  20.7 us (28%)
  Pallas kernels  8.19 us (11%)
  starting transfers between devices  4.39 us (6%)
  local copies, waits for them, and re-layouts  2.98 us (4%)
    all_to_all x1, blocking collectives, shards(): slices = lax.all_to_all(sent, CHIPS, 0, 0, tiled=True)  22.8 us
    all_to_all x1, blocking collectives, shards(): entering = lax.all_to_all(prefixes, CHIPS, 0, 0, tiled=True)  14.5 us
    ppermute x1, waiting for transfers between devices, shards(): below = lax.ppermute(to_up, 'head', ring('head', 1))  11.3 us
    pallas_call x9, Pallas kernels, call(): pl.pallas_call(body, out_shape=outs, in_specs=[HBM if i in fetched else V...  8.19 us
    ppermute x1, waiting for transfers between devices, shards(): far_up = lax.ppermute(far_a, 'head', ring('head', 1))  5.49 us
    unnamed x20, local copies, waits for them, and re-layouts  2.98 us
    ppermute x1, starting transfers between devices, shards(): far_down = lax.ppermute(far_b, 'head', ring('head', -1))  1.81 us
    ppermute x1, starting transfers between devices, shards(): above = lax.ppermute(to_down, 'head', ring('head', -1))  1.8 us
  transfers between devices with their start and end apart: 6, of which 5 were waited for; matrix products, arithmetic and copies ran while one was open for 0% of the time, Pallas kernels for 6%

profile of v3, /device:TPU:24, one launch (start us, length us, event | category | flops | bytes accessed | tf_op | source)
XLA Modules:
  0.0 73.7 jit_solution(2842084900283080705)
XLA Ops:
  0.0 1.0 %copy-done.1 = bf16[512,512]{1,0:T(8,128)(2,1)S(1)} copy-done((bf16[512,512]{1,0:T(8,128)(2,1)S(1)}, bf16[512,512]{1,0:T(8,128)(2,1)}, u32[]{:S(2)}) %copy-start.1) | copy-done | bytes 524312
  1.0 0.9 %copy-done.4 = bf16[512,256]{1,0:T(8,128)(2,1)S(1)} copy-done((bf16[512,256]{1,0:T(8,128)(2,1)S(1)}, bf16[512,256]{1,0:T(8,128)(2,1)}, u32[]{:S(2)}) %copy-start.4) | copy-done | bytes 262168
  2.0 0.9 %copy-done.6 = bf16[512,256]{1,0:T(8,128)(2,1)S(1)} copy-done((bf16[512,256]{1,0:T(8,128)(2,1)S(1)}, bf16[512,256]{1,0:T(8,128)(2,1)}, u32[]{:S(2)}) %copy-start.6) | copy-done | bytes 262168
  2.9 1.1 %shard_map.73 = (f32[512,128]{1,0:T(8,128)S(1)}, f32[8,128]{1,0:T(8,128)S(1)}, bf16[528,128]{1,0:T(8,128)(2,1)S(1)}) custom-call(bf16[512,256]{1,0:T(8,128)(2,1)S(1)} %copy-done.4, bf16[512,512]{1,0:T(8,128)(2,1)S(1)} %copy-done.1, bf16[512,256]{1,0:T(8,128)(2,1)S(1)} %copy-done.6), custom_call_target="tpu_custom_call" | custom-call | flops 1000000000 | bytes 1048576 | tf_op jit(solution)/shard_map/pallas_call | solution.py:26
  4.1 0.1 collective-permute-start
  4.2 1.3 %collective-permute-done.swap_ref = bf16[528,128]{1,0:T(8,128)(2,1)S(1)} collective-permute-done((bf16[528,128]{1,0:T(8,128)(2,1)S(1)}, bf16[528,128]{1,0:T(8,128)(2,1)S(1)}, u32[]{:S(2)}, u32[]{:S(2)}) %collective-permute-start) | collective-permute-done | bytes 135200 | tf_op jit(solution)/shard_map/ppermute | solution.py:268
  5.5 0.1 shard_map.74
  5.6 22.8 %all_to_all.10.in_ref = bf16[32,24,128]{2,1,0:T(8,128)(2,1)S(1)} all-to-all(bf16[32,24,128]{2,1,0:T(8,128)(2,1)S(1)} %get-tuple-element.27), channel_id=1, replica_groups=mesh['chip_x'=4,'chip_z'=8,'core'=2,'head'=4] {'chip_x','chip_z'}, dimensions={0} | all-to-all | bytes 393216 | tf_op jit(solution)/shard_map/all_to_all | solution.py:276
  28.4 0.1 shard_map.75
  28.5 14.5 %all_to_all.11.in_ref = bf16[32,16,128]{2,1,0:T(8,128)(2,1)S(1)} all-to-all(bf16[32,16,128]{2,1,0:T(8,128)(2,1)S(1)} %shard_map.75), channel_id=1, replica_groups=mesh['chip_x'=4,'chip_z'=8,'core'=2,'head'=4] {'chip_x','chip_z'}, dimensions={0} | all-to-all | bytes 262144 | tf_op jit(solution)/shard_map/all_to_all | solution.py:289
  43.1 0.1 collective-permute-start.1
  43.2 3.5 %shard_map.77 = (f32[512,512]{1,0:T(8,128)S(1)}, bf16[512,256]{1,0:T(8,128)(2,1)S(1)}, f32[512,512]{1,0:T(8,128)S(1)}) custom-call(bf16[512,256]{1,0:T(8,128)(2,1)S(1)} %copy-done.8, bf16[512,256]{1,0:T(8,128)(2,1)S(1)} %copy-done.5, bf16[512,512]{1,0:T(8,128)(2,1)S(1)} %copy-done.2, bf16[512,256]{1,0:T(8,128)(2,1)S(1)} %copy-done.7, ...), custom_call_target="tpu_custom_call" | custom-call | flops 1000000000 | bytes 1837056 | tf_op jit(solution)/shard_map/pallas_call | solution.py:26
  46.8 1.1 %shard_map.78 = (bf16[512,512]{1,0:T(8,128)(2,1)S(1)}, bf16[256,512]{1,0:T(8,128)(2,1)S(1)}, bf16[256,512]{1,0:T(8,128)(2,1)S(1)}) custom-call(bf16[512,128]{1,0:T(8,128)(2,1)S(1)} %get-tuple-element.30.keep_ref, bf16[512,128]{1,0:T(8,128)(2,1)S(1)} %collective-permute-done.1.other_ref, bf16[512,256]{1,0:T(8,128)(2,1)S(1)} %get-tuple-element.32.q_ref, ...), custom_call_target="tpu_custom_call" | custom-call | flops 1000000000 | bytes 4718592 | tf_op jit(solution)/shard_map/pallas_call | solution.py:26
  47.9 0.3 collective-permute-start.2
  48.2 1.8 %collective-permute-start.3 = (bf16[256,512]{1,0:T(8,128)(2,1)S(1)}, bf16[256,512]{1,0:T(8,128)(2,1)S(1)}, u32[]{:S(2)}, u32[]{:S(2)}) collective-permute-start(bf16[256,512]{1,0:T(8,128)(2,1)S(1)} %get-tuple-element.40), channel_id=1, source_target_pairs={{0,3},{1,0},{2,1},{3,2},{4,7},{5,4},{6,5},{7,6},{8,11},{9,8},{10,9... | collective-permute-start | bytes 786440 | tf_op jit(solution)/shard_map/ppermute | solution.py:307
  50.0 1.1 %shard_map.79 = (f32[512,512]{1,0:T(8,128)S(1)}, f32[512,512]{1,0:T(8,128)S(1)}, f32[512,512]{1,0:T(8,128)S(1)}) custom-call(bf16[512,512]{1,0:T(8,128)(2,1)S(1)} %get-tuple-element.35.gated_ref, bf16[512,2048]{1,0:T(8,128)(2,1)S(1)} %copy-done), custom_call_target="tpu_custom_call" | custom-call | flops 1000000000 | bytes 2621440 | tf_op jit(solution)/shard_map/pallas_call | solution.py:26
  51.2 5.5 %collective-permute-done.2.far_up_ref = bf16[256,512]{1,0:T(8,128)(2,1)S(1)} collective-permute-done((bf16[256,512]{1,0:T(8,128)(2,1)S(1)}, bf16[256,512]{1,0:T(8,128)(2,1)S(1)}, u32[]{:S(2)}, u32[]{:S(2)}) %collective-permute-start.2) | collective-permute-done | bytes 262176 | tf_op jit(solution)/shard_map/ppermute | solution.py:306
  56.6 1.3 %collective-permute-done.3.far_down_ref = bf16[256,512]{1,0:T(8,128)(2,1)S(1)} collective-permute-done((bf16[256,512]{1,0:T(8,128)(2,1)S(1)}, bf16[256,512]{1,0:T(8,128)(2,1)S(1)}, u32[]{:S(2)}, u32[]{:S(2)}) %collective-permute-start.3) | collective-permute-done | bytes 262176 | tf_op jit(solution)/shard_map/ppermute | solution.py:307
  57.9 0.1 shard_map.80
  58.1 0.3 collective-permute-start.4
  58.4 1.8 %collective-permute-start.5 = (bf16[512,512]{1,0:T(8,128)(2,1)S(1)}, bf16[512,512]{1,0:T(8,128)(2,1)S(1)}, u32[]{:S(2)}, u32[]{:S(2)}) collective-permute-start(bf16[512,512]{1,0:T(8,128)(2,1)S(1)} %get-tuple-element.42), channel_id=1, source_target_pairs={{0,3},{1,0},{2,1},{3,2},{4,7},{5,4},{6,5},{7,6},{8,11},{9,8},{10,9... | collective-permute-start | bytes 1572872 | tf_op jit(solution)/shard_map/ppermute | solution.py:313
  60.2 11.3 %collective-permute-done.4.below_ref = bf16[512,512]{1,0:T(8,128)(2,1)S(1)} collective-permute-done((bf16[512,512]{1,0:T(8,128)(2,1)S(1)}, bf16[512,512]{1,0:T(8,128)(2,1)S(1)}, u32[]{:S(2)}, u32[]{:S(2)}) %collective-permute-start.4) | collective-permute-done | bytes 524320 | tf_op jit(solution)/shard_map/ppermute | solution.py:312
  71.5 1.3 %collective-permute-done.5.above_ref = bf16[512,512]{1,0:T(8,128)(2,1)S(1)} collective-permute-done((bf16[512,512]{1,0:T(8,128)(2,1)S(1)}, bf16[512,512]{1,0:T(8,128)(2,1)S(1)}, u32[]{:S(2)}, u32[]{:S(2)}) %collective-permute-start.5) | collective-permute-done | bytes 524320 | tf_op jit(solution)/shard_map/ppermute | solution.py:313
  72.8 0.9 %shard_map.81 = bf16[512,512]{1,0:T(8,128)(2,1)} custom-call(f32[512,512]{1,0:T(8,128)S(1)} %get-tuple-element.36.own_ref, bf16[512,512]{1,0:T(8,128)(2,1)S(1)} %collective-permute-done.4.below_ref, bf16[512,512]{1,0:T(8,128)(2,1)S(1)} %collective-permute-done.5.above_ref), custom_call_target="tpu_custom_call" | custom-call | flops 1000000000 | bytes 2097152 | tf_op jit(solution)/shard_map/pallas_call | solution.py:26
  (19 shorter events, 0.1 us)
Async XLA Ops:
  0.0 1.0 %copy-start.1 = (bf16[512,512]{1,0:T(8,128)(2,1)S(1)}, bf16[512,512]{1,0:T(8,128)(2,1)}, u32[]{:S(2)}) copy-start(bf16[512,512]{1,0:T(8,128)(2,1)} %v_hbm.3) | copy-start | bytes 1572868
  1.0 0.9 %copy-start.4 = (bf16[512,256]{1,0:T(8,128)(2,1)S(1)}, bf16[512,256]{1,0:T(8,128)(2,1)}, u32[]{:S(2)}) copy-start(bf16[512,256]{1,0:T(8,128)(2,1)} %k_hbm.3) | copy-start | bytes 786436
  2.0 0.9 %copy-start.6 = (bf16[512,256]{1,0:T(8,128)(2,1)S(1)}, bf16[512,256]{1,0:T(8,128)(2,1)}, u32[]{:S(2)}) copy-start(bf16[512,256]{1,0:T(8,128)(2,1)} %g_hbm.3) | copy-start | bytes 786436
  4.1 1.4 %collective-permute-start = (bf16[528,128]{1,0:T(8,128)(2,1)S(1)}, bf16[528,128]{1,0:T(8,128)(2,1)S(1)}, u32[]{:S(2)}, u32[]{:S(2)}) collective-permute-start(bf16[528,128]{1,0:T(8,128)(2,1)S(1)} %get-tuple-element.26), channel_id=1, source_target_pairs={{0,4},{4,0},{1,5},{5,1},{2,6},{6,2},{3,7},{7,3},{8,12},{12,8},{9,1... | collective-permute-start | bytes 405512 | tf_op jit(solution)/shard_map/ppermute | solution.py:268
  28.5 14.7 %copy-start.2 = (bf16[512,512]{1,0:T(8,128)(2,1)S(1)}, bf16[512,512]{1,0:T(8,128)(2,1)}, u32[]{:S(2)}) copy-start(bf16[512,512]{1,0:T(8,128)(2,1)} %v_hbm.3) | copy-start | bytes 1572868
  28.5 14.7 %copy-start.3 = (bf16[512,512]{1,0:T(8,128)(2,1)S(1)}, bf16[512,512]{1,0:T(8,128)(2,1)}, u32[]{:S(2)}) copy-start(bf16[512,512]{1,0:T(8,128)(2,1)} %outer_hbm.1) | copy-start | bytes 1572868
  28.5 14.7 %copy-start.5 = (bf16[512,256]{1,0:T(8,128)(2,1)S(1)}, bf16[512,256]{1,0:T(8,128)(2,1)}, u32[]{:S(2)}) copy-start(bf16[512,256]{1,0:T(8,128)(2,1)} %k_hbm.3) | copy-start | bytes 786436
  28.5 14.7 %copy-start.7 = (bf16[512,256]{1,0:T(8,128)(2,1)S(1)}, bf16[512,256]{1,0:T(8,128)(2,1)}, u32[]{:S(2)}) copy-start(bf16[512,256]{1,0:T(8,128)(2,1)} %g_hbm.3) | copy-start | bytes 786436
  28.5 14.7 %copy-start.8 = (bf16[512,256]{1,0:T(8,128)(2,1)S(1)}, bf16[512,256]{1,0:T(8,128)(2,1)}, u32[]{:S(2)}) copy-start(bf16[512,256]{1,0:T(8,128)(2,1)} %q_hbm.1) | copy-start | bytes 786436
  28.5 14.7 %copy-start.9 = (f32[512]{0:T(512)S(1)}, f32[512]{0:T(512)}, u32[]{:S(2)}) copy-start(f32[512]{0:T(512)} %param.12) | copy-start | bytes 6148
  43.1 3.7 %copy-start = (bf16[512,2048]{1,0:T(8,128)(2,1)S(1)}, bf16[512,2048]{1,0:T(8,128)(2,1)}, u32[]{:S(2)}) copy-start(bf16[512,2048]{1,0:T(8,128)(2,1)} %w_hbm.3) | copy-start | bytes 6291460
  43.1 3.7 %collective-permute-start.1 = (bf16[512,128]{1,0:T(8,128)(2,1)S(1)}, bf16[512,128]{1,0:T(8,128)(2,1)S(1)}, u32[]{:S(2)}, u32[]{:S(2)}) collective-permute-start(bf16[512,128]{1,0:T(8,128)(2,1)S(1)} %get-tuple-element.31), channel_id=1, source_target_pairs={{0,4},{4,0},{1,5},{5,1},{2,6},{6,2},{3,7},{7,3},{8,12},{12,8},{9,1... | collective-permute-start | bytes 393224 | tf_op jit(solution)/shard_map/ppermute | solution.py:292
  47.9 8.7 %collective-permute-start.2 = (bf16[256,512]{1,0:T(8,128)(2,1)S(1)}, bf16[256,512]{1,0:T(8,128)(2,1)S(1)}, u32[]{:S(2)}, u32[]{:S(2)}) collective-permute-start(bf16[256,512]{1,0:T(8,128)(2,1)S(1)} %get-tuple-element.39), channel_id=1, source_target_pairs={{0,1},{1,2},{2,3},{3,0},{4,5},{5,6},{6,7},{7,4},{8,9},{9,10},{10,1... | collective-permute-start | bytes 786440 | tf_op jit(solution)/shard_map/ppermute | solution.py:306
  48.2 9.8 %collective-permute-start.3 = (bf16[256,512]{1,0:T(8,128)(2,1)S(1)}, bf16[256,512]{1,0:T(8,128)(2,1)S(1)}, u32[]{:S(2)}, u32[]{:S(2)}) collective-permute-start(bf16[256,512]{1,0:T(8,128)(2,1)S(1)} %get-tuple-element.40), channel_id=1, source_target_pairs={{0,3},{1,0},{2,1},{3,2},{4,7},{5,4},{6,5},{7,6},{8,11},{9,8},{10,9... | collective-permute-start | bytes 786440 | tf_op jit(solution)/shard_map/ppermute | solution.py:307
  58.1 13.4 %collective-permute-start.4 = (bf16[512,512]{1,0:T(8,128)(2,1)S(1)}, bf16[512,512]{1,0:T(8,128)(2,1)S(1)}, u32[]{:S(2)}, u32[]{:S(2)}) collective-permute-start(bf16[512,512]{1,0:T(8,128)(2,1)S(1)} %get-tuple-element.41), channel_id=1, source_target_pairs={{0,1},{1,2},{2,3},{3,0},{4,5},{5,6},{6,7},{7,4},{8,9},{9,10},{10,1... | collective-permute-start | bytes 1572872 | tf_op jit(solution)/shard_map/ppermute | solution.py:312
  58.4 14.4 %collective-permute-start.5 = (bf16[512,512]{1,0:T(8,128)(2,1)S(1)}, bf16[512,512]{1,0:T(8,128)(2,1)S(1)}, u32[]{:S(2)}, u32[]{:S(2)}) collective-permute-start(bf16[512,512]{1,0:T(8,128)(2,1)S(1)} %get-tuple-element.42), channel_id=1, source_target_pairs={{0,3},{1,0},{2,1},{3,2},{4,7},{5,4},{6,5},{7,6},{8,11},{9,8},{10,9... | collective-permute-start | bytes 1572872 | tf_op jit(solution)/shard_map/ppermute | solution.py:313

commit v4 on v3

--- a/solution.py
+++ b/solution.py
@@ -18,11 +18,17 @@
 HBM = pl.BlockSpec(memory_space=pltpu.HBM)
 
 
-def call(body, outs, *args, fetched=(), flops=10**9):
+def call(body, outs, *args, fetched=(), pieces=0, flops=10**9):
     moved = sum(a.size * a.dtype.itemsize for a in args)
+    args = [
+        pltpu.with_memory_space_constraint(a, pltpu.HBM) if i in fetched else a
+        for i, a in enumerate(args)
+    ]
     scratch = [pltpu.VMEM(args[i].shape, args[i].dtype) for i in fetched]
+    if pieces:
+        scratch = [pltpu.VMEM((pieces, DV, DV), BF16)]
     if fetched:
-        scratch.append(pltpu.SemaphoreType.DMA((len(fetched),)))
+        scratch.append(pltpu.SemaphoreType.DMA((max(pieces, len(fetched)),)))
     return pl.pallas_call(
         body,
         out_shape=outs,
@@ -106,7 +112,7 @@
         first = jnp.where(early, own, other)
         second = jnp.where(early, other, own)
         state = first * jnp.exp(jnp.where(early, other_log, own_log)) + second
-        first_ref[at, :] = first
+        first_ref[at, :] = first.astype(BF16)
         decays.append(jnp.exp(jnp.where(early, own_log, other_log)))
         sums.append(own_log + other_log)
         piece = slice(side * rows, (side + 1) * rows)
@@ -137,7 +143,7 @@
         at = slice(side * half, (side + 1) * half)
         piece = slice(side * rows, (side + 1) * rows)
         entering = in_ref[:, piece, :].astype(F32).reshape(half, LANE)
-        between = entering * decay_ref[side : side + 1, :] + first_ref[at, :]
+        between = entering * decay_ref[side : side + 1, :] + first_ref[at, :].astype(F32)
         keep_ref[at, :] = jnp.where(early, entering, between).astype(BF16)
         send_ref[at, :] = jnp.where(early, between, entering).astype(BF16)
 
@@ -182,24 +188,35 @@
             block = dot(k_state, value)
             carried = block if i == 0 else carried * jnp.exp(ending).reshape(DK, 1) + block
         outer_f = outer_ref[at, :].astype(F32)
-        scale_ref[at, :] = outer_f / (1.0 + jnp.exp(-outer_f)) * gain_ref[...]
+        scale = outer_f / (1.0 + jnp.exp(-outer_f)) * gain_ref[...]
+        scale_ref[at, :] = scale.astype(BF16)
 
 
 def columns(index, width):
     return pl.ds(pl.multiple_of(index * width, width), width)
 
 
+def head_columns(shift, width):
+    count = lax.axis_size("head")
+    return columns(lax.rem(lax.axis_index("head") + shift, count), width)
+
+
+def fetch_columns(w_hbm, w_ref, sems, *shifts):
+    width = w_ref.shape[-1]
+    copies = [
+        pltpu.make_async_copy(w_hbm.at[:, head_columns(shift, width)], w_ref.at[i], sems.at[i])
+        for i, shift in enumerate(shifts)
+    ]
+    for copy in copies:
+        copy.start()
+    return copies
+
+
 def finish_body(
-    keep_ref, other_ref, q_ref, att_ref, scale_ref, w_hbm, gated_ref, far_a_ref, far_b_ref,
+    keep_ref, other_ref, q_ref, att_ref, scale_ref, w_hbm, gated_ref, far_up_ref, far_down_ref,
     w_ref, sems,
 ):
-    count = lax.axis_size("head")
-    width = far_a_ref.shape[1]
-    far = lax.rem(lax.axis_index("head") + count // 2, count)
-    copy = pltpu.make_async_copy(
-        w_hbm.at[:, columns(far, width)], w_ref.at[:, columns(0, width)], sems.at[0]
-    )
-    copy.start()
+    (copy,) = fetch_columns(w_hbm, w_ref, sems, 2)
     half = DV // 2
     core = lax.axis_index("core")
     total = 0.0
@@ -213,36 +230,47 @@
     inverse = lax.rsqrt(total * (1.0 / DV) + 1e-05)
     for attention, place in parts:
         at = columns(place, half)
-        gated_ref[:, at] = (attention * inverse * scale_ref[:, at]).astype(BF16)
+        scale = scale_ref[:, at].astype(F32)
+        gated_ref[:, at] = (attention * inverse * scale).astype(BF16)
+    rows = far_up_ref.shape[0]
     copy.wait()
-    rows = far_a_ref.shape[0]
-    weight = w_ref[:, 0:width]
-    far_a_ref[...] = dot(gated_ref[:rows, :], weight).astype(BF16)
-    far_b_ref[...] = dot(gated_ref[rows:, :], weight).astype(BF16)
+    far_up_ref[...] = dot(gated_ref[:rows, :], w_ref[0]).astype(BF16)
+    far_down_ref[...] = dot(gated_ref[rows:, :], w_ref[0]).astype(BF16)
+
+
+def direct_body(gated_ref, w_hbm, up_ref, down_ref, w_ref, sems):
+    copies = fetch_columns(w_hbm, w_ref, sems, 1, 3)
+    rows = up_ref.shape[0]
+    copies[0].wait()
+    up_ref[...] = dot(gated_ref[rows:, :], w_ref[0]).astype(BF16)
+    copies[1].wait()
+    down_ref[...] = dot(gated_ref[:rows, :], w_ref[1]).astype(BF16)
 
 
 def near_body(gated_ref, w_hbm, up_ref, down_ref, own_ref, w_ref, sems):
-    count = lax.axis_size("head")
-    width = own_ref.shape[1]
-    me = lax.axis_index("head")
-    copy = pltpu.make_async_copy(w_hbm, w_ref, sems.at[0])
-    copy.start()
-    copy.wait()
-    for ref, shift in ((up_ref, 1), (down_ref, count - 1), (own_ref, 0)):
-        ref[...] = dot(gated_ref[...], w_ref[:, columns(lax.rem(me + shift, count), width)])
+    copies = fetch_columns(w_hbm, w_ref, sems, 1, 3, 0)
+    rows = up_ref.shape[0]
+    copies[0].wait()
+    up_ref[...] = dot(gated_ref[:rows, :], w_ref[0])
+    copies[1].wait()
+    down_ref[...] = dot(gated_ref[rows:, :], w_ref[1])
+    copies[2].wait()
+    own_ref[...] = dot(gated_ref[...], w_ref[2])
 
 
 def pass_body(up_ref, down_ref, far_up_ref, far_down_ref, up_out_ref, down_out_ref):
-    rows = far_up_ref.shape[0]
-    up_out_ref[:rows, :] = (up_ref[:rows, :] + far_up_ref[...].astype(F32)).astype(BF16)
-    up_out_ref[rows:, :] = up_ref[rows:, :].astype(BF16)
-    down_out_ref[:rows, :] = down_ref[:rows, :].astype(BF16)
-    down_out_ref[rows:, :] = (down_ref[rows:, :] + far_down_ref[...].astype(F32)).astype(BF16)
-
-
-def sum_body(own_ref, below_ref, above_ref, out_ref):
-    total = own_ref[...] + below_ref[...].astype(F32) + above_ref[...].astype(F32)
-    out_ref[...] = total.astype(BF16)
+    up_out_ref[...] = (up_ref[...] + far_up_ref[...].astype(F32)).astype(BF16)
+    down_out_ref[...] = (down_ref[...] + far_down_ref[...].astype(F32)).astype(BF16)
+
+
+def sum_body(own_ref, below_a_ref, below_b_ref, above_a_ref, above_b_ref, out_ref):
+    rows = below_a_ref.shape[0]
+    for at, below, above in (
+        (slice(0, rows), below_a_ref, above_a_ref),
+        (slice(rows, 2 * rows), below_b_ref, above_b_ref),
+    ):
+        total = own_ref[at, :] + below[...].astype(F32) + above[...].astype(F32)
+        out_ref[at, :] = total.astype(BF16)
 
 
 def ring(axis, shift):
@@ -268,7 +296,7 @@
     swapped = lax.ppermute(swap, "core", ring("core", 1))
     sent, first, decay = call(
         join_body,
-        (shape((pieces, 2 * rows + 8, LANE), BF16), shape((DV, LANE), F32), small),
+        (shape((pieces, 2 * rows + 8, LANE), BF16), shape((DV, LANE), BF16), small),
         own,
         own_log,
         swapped,
@@ -276,7 +304,7 @@
     slices = lax.all_to_all(sent, CHIPS, 0, 0, tiled=True)
     att_local, q_start, scale = call(
         local_body,
-        (shape((length, DV), F32), shape((length, DK), BF16), shape((length, DV), F32)),
+        (shape((length, DV), F32), shape((length, DK), BF16), shape((length, DV), BF16)),
         queries,
         key_vectors,
         values,
@@ -288,11 +316,15 @@
     prefixes = call(scan_body, shape((pieces, 2 * rows, LANE), BF16), slices)
     entering = lax.all_to_all(prefixes, CHIPS, 0, 0, tiled=True)
     state_half = shape((DV, LANE), BF16)
+    entering, att_local, q_start, scale = lax.optimization_barrier(
+        (entering, att_local, q_start, scale)
+    )
     keep, send = call(part_body, (state_half, state_half), entering, first, decay)
     other = lax.ppermute(send, "core", ring("core", 1))
     width = out_weight.shape[1] // lax.axis_size("head")
     near = shape((length // 2, width), BF16)
-    gated, far_a, far_b = call(
+    near_f = shape((length // 2, width), F32)
+    gated, far_up, far_down = call(
         finish_body,
         (shape((length, DV), BF16), near, near),
         keep,
@@ -302,16 +334,30 @@
         scale,
         out_weight,
         fetched=(5,),
-    )
-    far_up = lax.ppermute(far_a, "head", ring("head", 1))
-    far_down = lax.ppermute(far_b, "head", ring("head", -1))
-    block = shape((length, width), F32)
-    up, down, own_part = call(near_body, (block, block, block), gated, out_weight, fetched=(1,))
-    block = shape((length, width), BF16)
-    to_up, to_down = call(pass_body, (block, block), up, down, far_up, far_down)
-    below = lax.ppermute(to_up, "head", ring("head", 1))
-    above = lax.ppermute(to_down, "head", ring("head", -1))
-    return call(sum_body, block, own_part, below, above)
+        pieces=1,
+    )
+    up, down = ring("head", 1), ring("head", -1)
+    far_up = lax.ppermute(far_up, "head", up)
+    far_down = lax.ppermute(far_down, "head", down)
+    up_b, down_a = call(
+        direct_body, (near, near), gated, out_weight, fetched=(1,), pieces=2
+    )
+    below_b = lax.ppermute(up_b, "head", up)
+    above_a = lax.ppermute(down_a, "head", down)
+    up_a, down_b, own_part = call(
+        near_body,
+        (near_f, near_f, shape((length, width), F32)),
+        gated,
+        out_weight,
+        fetched=(1,),
+        pieces=3,
+    )
+    up_a, down_b = call(pass_body, (near, near), up_a, down_b, far_up, far_down)
+    below_a = lax.ppermute(up_a, "head", up)
+    above_b = lax.ppermute(down_b, "head", down)
+    return call(
+        sum_body, shape((length, width), BF16), own_part, below_a, below_b, above_a, above_b
+    )
 
 
 def solution(mesh):

time: 74 us -> 67.6 us (0.914)
  blocking collectives: 37.3 us -> 22.8 us
  Pallas kernels: 8.19 us -> 14.4 us
  starting transfers between devices: 4.39 us -> 10.6 us
  local copies, waits for them, and re-layouts: 2.98 us -> 0.01 us
  waiting for transfers between devices: 20.7 us -> 19.1 us
    all_to_all x1 -> x0, blocking collectives: 14.5 us -> none  [shards(): entering = lax.all_to_all(prefixes, CHIPS, 0, 0, tiled=True)]
    ppermute x4 -> x6, waiting for transfers between devices: 19.4 us -> 10.8 us  [the longest x1 3.37 us: shards(): below_a = lax.ppermute(up_a, 'head', up)]
    pallas_call x9 -> x10, Pallas kernels: 8.19 us -> 14.4 us  [call(): pl.pallas_call(body, out_shape=outs, in_specs=[HBM if i in fetched else V...]
    all_to_all x0 -> x1, waiting for transfers between devices: none -> 5.6 us  [shards(): entering = lax.all_to_all(prefixes, CHIPS, 0, 0, tiled=True)]
    all_to_all x0 -> x1, starting transfers between devices: none -> 4.09 us  [shards(): entering = lax.all_to_all(prefixes, CHIPS, 0, 0, tiled=True)]
    unnamed x20 -> x2, local copies, waits for them, and re-layouts: 2.98 us -> 0.01 us
    ppermute x4 -> x6, starting transfers between devices: 4.21 us -> 6.31 us  [the longest x1 1.8 us: shards(): far_down = lax.ppermute(far_down, 'head', down)]
    ppermute x1, waiting for transfers between devices: 0.01 us -> 1.33 us  [shards(): other = lax.ppermute(send, 'core', ring('core', 1))]
  transfers between devices with their start and end apart: 6 -> 9, of which waited for: 5 -> 9; matrix products, arithmetic and copies ran while one was open for 0% -> 0% of each run, Pallas kernels for 6% -> 13%
where the time goes in v4:
time: 67.6 us; the launch traced here: 67 us
  blocking collectives  22.8 us (34%)
  waiting for transfers between devices  19.1 us (28%)
  Pallas kernels  14.4 us (21%)
  starting transfers between devices  10.6 us (16%)
    all_to_all x1, blocking collectives, shards(): slices = lax.all_to_all(sent, CHIPS, 0, 0, tiled=True)  22.8 us
    pallas_call x10, Pallas kernels, call(): pl.pallas_call(body, out_shape=outs, in_specs=[HBM if i in fetched else V...  14.4 us
    all_to_all x1, waiting for transfers between devices, shards(): entering = lax.all_to_all(prefixes, CHIPS, 0, 0, tiled=True)  5.6 us
    all_to_all x1, starting transfers between devices, shards(): entering = lax.all_to_all(prefixes, CHIPS, 0, 0, tiled=True)  4.09 us
    ppermute x1, waiting for transfers between devices, shards(): below_a = lax.ppermute(up_a, 'head', up)  3.37 us
    ppermute x1, waiting for transfers between devices, shards(): below_b = lax.ppermute(up_b, 'head', up)  1.99 us
    ppermute x1, starting transfers between devices, shards(): far_down = lax.ppermute(far_down, 'head', down)  1.8 us
    ppermute x1, starting transfers between devices, shards(): above_b = lax.ppermute(down_b, 'head', down)  1.66 us
  transfers between devices with their start and end apart: 9, of which 9 were waited for; matrix products, arithmetic and copies ran while one was open for 0% of the time, Pallas kernels for 13%

profile of v4, /device:TPU:24, one launch (start us, length us, event | category | flops | bytes accessed | tf_op | source)
XLA Modules:
  0.0 67.0 jit_solution(6161441588228654900)
XLA Ops:
  0.0 1.9 %shard_map.73 = (f32[512,128]{1,0:T(8,128)S(1)}, f32[8,128]{1,0:T(8,128)S(1)}, bf16[528,128]{1,0:T(8,128)(2,1)S(1)}) custom-call(bf16[512,256]{1,0:T(8,128)(2,1)} %k_hbm.3, bf16[512,512]{1,0:T(8,128)(2,1)} %v_hbm.3, bf16[512,256]{1,0:T(8,128)(2,1)} %g_hbm.3), custom_call_target="tpu_custom_call" | custom-call | flops 1000000000 | bytes 1048576 | tf_op jit(solution)/shard_map/pallas_call | solution.py:32
  2.1 1.3 %collective-permute-done.swap_ref = bf16[528,128]{1,0:T(8,128)(2,1)S(1)} collective-permute-done((bf16[528,128]{1,0:T(8,128)(2,1)S(1)}, bf16[528,128]{1,0:T(8,128)(2,1)S(1)}, u32[]{:S(2)}, u32[]{:S(2)}) %collective-permute-start) | collective-permute-done | bytes 135200 | tf_op jit(solution)/shard_map/ppermute | solution.py:296
  3.5 22.8 %all_to_all.10.in_ref = bf16[32,24,128]{2,1,0:T(8,128)(2,1)S(1)} all-to-all(bf16[32,24,128]{2,1,0:T(8,128)(2,1)S(1)} %get-tuple-element.33), channel_id=1, replica_groups=mesh['chip_x'=4,'chip_z'=8,'core'=2,'head'=4] {'chip_x','chip_z'}, dimensions={0} | all-to-all | bytes 393216 | tf_op jit(solution)/shard_map/all_to_all | solution.py:304
  26.3 0.7 %shard_map.75 = bf16[32,16,128]{2,1,0:T(8,128)(2,1)} custom-call(bf16[32,24,128]{2,1,0:T(8,128)(2,1)S(1)} %all_to_all.10.in_ref), custom_call_target="tpu_custom_call" | custom-call | flops 1000000000 | bytes 196608 | tf_op jit(solution)/shard_map/pallas_call | solution.py:32
  27.0 4.1 %all-to-all-start.1 = ((bf16[32,16,128]{2,1,0:T(8,128)(2,1)}), bf16[32,16,128]{2,1,0:T(8,128)(2,1)S(1)}, u32[]{:S(2)}, u32[]{:S(2)}) async-start(bf16[32,16,128]{2,1,0:T(8,128)(2,1)} %shard_map.75), calls=%async_computation.1 | async-start | bytes 262144 | tf_op jit(solution)/shard_map/all_to_all | solution.py:317
  31.1 4.8 %shard_map.76 = (f32[512,512]{1,0:T(8,128)S(1)}, bf16[512,256]{1,0:T(8,128)(2,1)S(1)}, bf16[512,512]{1,0:T(8,128)(2,1)S(1)}) custom-call(bf16[512,256]{1,0:T(8,128)(2,1)} %q_hbm.1, bf16[512,256]{1,0:T(8,128)(2,1)} %k_hbm.3, bf16[512,512]{1,0:T(8,128)(2,1)} %v_hbm.3, bf16[512,256]{1,0:T(8,128)(2,1)} %g_hbm.3, bf16[512,512]{1,0:T(8,128)(2,1)} %outer_hbm.1, ...), custom_call_target="tpu_custom_call" | custom-call | flops 1000000000 | bytes 1837056 | tf_op jit(solution)/shard_map/pallas_call | solution.py:32
  36.0 5.6 %all-to-all-done.1.in_ref = bf16[32,16,128]{2,1,0:T(8,128)(2,1)S(1)} async-done(((bf16[32,16,128]{2,1,0:T(8,128)(2,1)}), bf16[32,16,128]{2,1,0:T(8,128)(2,1)S(1)}, u32[]{:S(2)}, u32[]{:S(2)}) %all-to-all-start.1) | async-done | bytes 131104 | tf_op jit(solution)/shard_map/all_to_all | solution.py:317
  41.7 1.3 %collective-permute-done.1.other_ref = bf16[512,128]{1,0:T(8,128)(2,1)S(1)} collective-permute-done((bf16[512,128]{1,0:T(8,128)(2,1)S(1)}, bf16[512,128]{1,0:T(8,128)(2,1)S(1)}, u32[]{:S(2)}, u32[]{:S(2)}) %collective-permute-start.1) | collective-permute-done | bytes 131104 | tf_op jit(solution)/shard_map/ppermute | solution.py:323
  43.1 2.0 %shard_map.78 = (bf16[512,512]{1,0:T(8,128)(2,1)S(1)}, bf16[256,512]{1,0:T(8,128)(2,1)S(1)}, bf16[256,512]{1,0:T(8,128)(2,1)S(1)}) custom-call(bf16[512,128]{1,0:T(8,128)(2,1)S(1)} %get-tuple-element.40.keep_ref, bf16[512,128]{1,0:T(8,128)(2,1)S(1)} %collective-permute-done.1.other_ref, bf16[512,256]{1,0:T(8,128)(2,1)S(1)} %get-tuple-element.42.q_ref, ...), custom_call_target="tpu_custom_call" | custom-call | flops 1000000000 | bytes 4194304 | tf_op jit(solution)/shard_map/pallas_call | solution.py:32
  45.1 0.3 collective-permute-start.2
  45.4 1.8 %collective-permute-start.3 = (bf16[256,512]{1,0:T(8,128)(2,1)S(1)}, bf16[256,512]{1,0:T(8,128)(2,1)S(1)}, u32[]{:S(2)}, u32[]{:S(2)}) collective-permute-start(bf16[256,512]{1,0:T(8,128)(2,1)S(1)} %get-tuple-element.50), channel_id=1, source_target_pairs={{0,3},{1,0},{2,1},{3,2},{4,7},{5,4},{6,5},{7,6},{8,11},{9,8},{10,9... | collective-permute-start | bytes 786440 | tf_op jit(solution)/shard_map/ppermute | solution.py:341
  47.2 1.7 %shard_map.81 = (bf16[256,512]{1,0:T(8,128)(2,1)S(1)}, bf16[256,512]{1,0:T(8,128)(2,1)S(1)}) custom-call(bf16[512,512]{1,0:T(8,128)(2,1)S(1)} %get-tuple-element.45.gated_ref, bf16[512,2048]{1,0:T(8,128)(2,1)} %w_hbm.5), custom_call_target="tpu_custom_call" | custom-call | flops 1000000000 | bytes 2621440 | tf_op jit(solution)/shard_map/pallas_call | solution.py:32
  48.8 1.5 %collective-permute-start.5 = (bf16[256,512]{1,0:T(8,128)(2,1)S(1)}, bf16[256,512]{1,0:T(8,128)(2,1)S(1)}, u32[]{:S(2)}, u32[]{:S(2)}) collective-permute-start(bf16[256,512]{1,0:T(8,128)(2,1)S(1)} %get-tuple-element.52), channel_id=1, source_target_pairs={{0,1},{1,2},{2,3},{3,0},{4,5},{5,6},{6,7},{7,4},{8,9},{9,10},{10,1... | collective-permute-start | bytes 786440 | tf_op jit(solution)/shard_map/ppermute | solution.py:345
  50.3 0.6 collective-permute-start.6
  50.9 2.1 %shard_map.79 = (f32[256,512]{1,0:T(8,128)S(1)}, f32[256,512]{1,0:T(8,128)S(1)}, f32[512,512]{1,0:T(8,128)S(1)}) custom-call(bf16[512,512]{1,0:T(8,128)(2,1)S(1)} %get-tuple-element.45.gated_ref, bf16[512,2048]{1,0:T(8,128)(2,1)} %w_hbm.5), custom_call_target="tpu_custom_call" | custom-call | flops 1000000000 | bytes 2621440 | tf_op jit(solution)/shard_map/pallas_call | solution.py:32
  53.1 1.3 %collective-permute-done.2.far_up_ref = bf16[256,512]{1,0:T(8,128)(2,1)S(1)} collective-permute-done((bf16[256,512]{1,0:T(8,128)(2,1)S(1)}, bf16[256,512]{1,0:T(8,128)(2,1)S(1)}, u32[]{:S(2)}, u32[]{:S(2)}) %collective-permute-start.2) | collective-permute-done | bytes 262176 | tf_op jit(solution)/shard_map/ppermute | solution.py:340
  54.3 1.4 %collective-permute-done.3.far_down_ref = bf16[256,512]{1,0:T(8,128)(2,1)S(1)} collective-permute-done((bf16[256,512]{1,0:T(8,128)(2,1)S(1)}, bf16[256,512]{1,0:T(8,128)(2,1)S(1)}, u32[]{:S(2)}, u32[]{:S(2)}) %collective-permute-start.3) | collective-permute-done | bytes 262176 | tf_op jit(solution)/shard_map/ppermute | solution.py:341
  55.8 0.4 collective-permute-start.4
  56.3 1.7 %collective-permute-start.7 = (bf16[256,512]{1,0:T(8,128)(2,1)S(1)}, bf16[256,512]{1,0:T(8,128)(2,1)S(1)}, u32[]{:S(2)}, u32[]{:S(2)}) collective-permute-start(bf16[256,512]{1,0:T(8,128)(2,1)S(1)} %get-tuple-element.54), channel_id=1, source_target_pairs={{0,3},{1,0},{2,1},{3,2},{4,7},{5,4},{6,5},{7,6},{8,11},{9,8},{10,9... | collective-permute-start | bytes 786440 | tf_op jit(solution)/shard_map/ppermute | solution.py:357
  57.9 2.0 %collective-permute-done.5.below_b_ref = bf16[256,512]{1,0:T(8,128)(2,1)S(1)} collective-permute-done((bf16[256,512]{1,0:T(8,128)(2,1)S(1)}, bf16[256,512]{1,0:T(8,128)(2,1)S(1)}, u32[]{:S(2)}, u32[]{:S(2)}) %collective-permute-start.5) | collective-permute-done | bytes 262176 | tf_op jit(solution)/shard_map/ppermute | solution.py:345
  59.9 1.4 %collective-permute-done.6.above_a_ref = bf16[256,512]{1,0:T(8,128)(2,1)S(1)} collective-permute-done((bf16[256,512]{1,0:T(8,128)(2,1)S(1)}, bf16[256,512]{1,0:T(8,128)(2,1)S(1)}, u32[]{:S(2)}, u32[]{:S(2)}) %collective-permute-start.6) | collective-permute-done | bytes 262176 | tf_op jit(solution)/shard_map/ppermute | solution.py:346
  61.4 3.4 %collective-permute-done.4.below_a_ref = bf16[256,512]{1,0:T(8,128)(2,1)S(1)} collective-permute-done((bf16[256,512]{1,0:T(8,128)(2,1)S(1)}, bf16[256,512]{1,0:T(8,128)(2,1)S(1)}, u32[]{:S(2)}, u32[]{:S(2)}) %collective-permute-start.4) | collective-permute-done | bytes 262176 | tf_op jit(solution)/shard_map/ppermute | solution.py:356
  64.7 1.3 %collective-permute-done.7.above_b_ref = bf16[256,512]{1,0:T(8,128)(2,1)S(1)} collective-permute-done((bf16[256,512]{1,0:T(8,128)(2,1)S(1)}, bf16[256,512]{1,0:T(8,128)(2,1)S(1)}, u32[]{:S(2)}, u32[]{:S(2)}) %collective-permute-start.7) | collective-permute-done | bytes 262176 | tf_op jit(solution)/shard_map/ppermute | solution.py:357
  66.0 0.9 %shard_map.82 = bf16[512,512]{1,0:T(8,128)(2,1)} custom-call(f32[512,512]{1,0:T(8,128)S(1)} %get-tuple-element.46.own_ref, bf16[256,512]{1,0:T(8,128)(2,1)S(1)} %collective-permute-done.4.below_a_ref, bf16[256,512]{1,0:T(8,128)(2,1)S(1)} %collective-permute-done.5.below_b_ref, bf16[256,512]{1,0:T(8,128)(2,1)S(1)} %collective-permute-done.6.above_a_ref, ...), custom_call_target="tpu_custom_call" | custom-call | flops 1000000000 | bytes 2097152 | tf_op jit(solution)/shard_map/pallas_call | solution.py:32
  (7 shorter events, 0.4 us)
Async XLA Ops:
  2.0 1.4 %collective-permute-start = (bf16[528,128]{1,0:T(8,128)(2,1)S(1)}, bf16[528,128]{1,0:T(8,128)(2,1)S(1)}, u32[]{:S(2)}, u32[]{:S(2)}) collective-permute-start(bf16[528,128]{1,0:T(8,128)(2,1)S(1)} %get-tuple-element.32), channel_id=1, source_target_pairs={{0,4},{4,0},{1,5},{5,1},{2,6},{6,2},{3,7},{7,3},{8,12},{12,8},{9,1... | collective-permute-start | bytes 405512 | tf_op jit(solution)/shard_map/ppermute | solution.py:296
  3.5 27.6 %copy-start = (f32[512]{0:T(512)S(1)}, f32[512]{0:T(512)}, u32[]{:S(2)}) copy-start(f32[512]{0:T(512)} %param.12) | copy-start | bytes 6148
  27.0 14.5 %all-to-all-start.1 = ((bf16[32,16,128]{2,1,0:T(8,128)(2,1)}), bf16[32,16,128]{2,1,0:T(8,128)(2,1)S(1)}, u32[]{:S(2)}, u32[]{:S(2)}) async-start(bf16[32,16,128]{2,1,0:T(8,128)(2,1)} %shard_map.75), calls=%async_computation.1 | async-start | bytes 262144 | tf_op jit(solution)/shard_map/all_to_all | solution.py:317
  41.6 1.4 %collective-permute-start.1 = (bf16[512,128]{1,0:T(8,128)(2,1)S(1)}, bf16[512,128]{1,0:T(8,128)(2,1)S(1)}, u32[]{:S(2)}, u32[]{:S(2)}) collective-permute-start(bf16[512,128]{1,0:T(8,128)(2,1)S(1)} %get-tuple-element.41), channel_id=1, source_target_pairs={{0,4},{4,0},{1,5},{5,1},{2,6},{6,2},{3,7},{7,3},{8,12},{12,8},{9,1... | collective-permute-start | bytes 393224 | tf_op jit(solution)/shard_map/ppermute | solution.py:323
  45.1 9.3 %collective-permute-start.2 = (bf16[256,512]{1,0:T(8,128)(2,1)S(1)}, bf16[256,512]{1,0:T(8,128)(2,1)S(1)}, u32[]{:S(2)}, u32[]{:S(2)}) collective-permute-start(bf16[256,512]{1,0:T(8,128)(2,1)S(1)} %get-tuple-element.49), channel_id=1, source_target_pairs={{0,1},{1,2},{2,3},{3,0},{4,5},{5,6},{6,7},{7,4},{8,9},{9,10},{10,1... | collective-permute-start | bytes 786440 | tf_op jit(solution)/shard_map/ppermute | solution.py:340
  45.4 10.4 %collective-permute-start.3 = (bf16[256,512]{1,0:T(8,128)(2,1)S(1)}, bf16[256,512]{1,0:T(8,128)(2,1)S(1)}, u32[]{:S(2)}, u32[]{:S(2)}) collective-permute-start(bf16[256,512]{1,0:T(8,128)(2,1)S(1)} %get-tuple-element.50), channel_id=1, source_target_pairs={{0,3},{1,0},{2,1},{3,2},{4,7},{5,4},{6,5},{7,6},{8,11},{9,8},{10,9... | collective-permute-start | bytes 786440 | tf_op jit(solution)/shard_map/ppermute | solution.py:341
  48.8 11.1 %collective-permute-start.5 = (bf16[256,512]{1,0:T(8,128)(2,1)S(1)}, bf16[256,512]{1,0:T(8,128)(2,1)S(1)}, u32[]{:S(2)}, u32[]{:S(2)}) collective-permute-start(bf16[256,512]{1,0:T(8,128)(2,1)S(1)} %get-tuple-element.52), channel_id=1, source_target_pairs={{0,1},{1,2},{2,3},{3,0},{4,5},{5,6},{6,7},{7,4},{8,9},{9,10},{10,1... | collective-permute-start | bytes 786440 | tf_op jit(solution)/shard_map/ppermute | solution.py:345
  50.3 11.0 %collective-permute-start.6 = (bf16[256,512]{1,0:T(8,128)(2,1)S(1)}, bf16[256,512]{1,0:T(8,128)(2,1)S(1)}, u32[]{:S(2)}, u32[]{:S(2)}) collective-permute-start(bf16[256,512]{1,0:T(8,128)(2,1)S(1)} %get-tuple-element.53), channel_id=1, source_target_pairs={{0,3},{1,0},{2,1},{3,2},{4,7},{5,4},{6,5},{7,6},{8,11},{9,8},{10,9... | collective-permute-start | bytes 786440 | tf_op jit(solution)/shard_map/ppermute | solution.py:346
  55.8 8.9 %collective-permute-start.4 = (bf16[256,512]{1,0:T(8,128)(2,1)S(1)}, bf16[256,512]{1,0:T(8,128)(2,1)S(1)}, u32[]{:S(2)}, u32[]{:S(2)}) collective-permute-start(bf16[256,512]{1,0:T(8,128)(2,1)S(1)} %get-tuple-element.51), channel_id=1, source_target_pairs={{0,1},{1,2},{2,3},{3,0},{4,5},{5,6},{6,7},{7,4},{8,9},{9,10},{10,1... | collective-permute-start | bytes 786440 | tf_op jit(solution)/shard_map/ppermute | solution.py:356
  56.3 9.8 %collective-permute-start.7 = (bf16[256,512]{1,0:T(8,128)(2,1)S(1)}, bf16[256,512]{1,0:T(8,128)(2,1)S(1)}, u32[]{:S(2)}, u32[]{:S(2)}) collective-permute-start(bf16[256,512]{1,0:T(8,128)(2,1)S(1)} %get-tuple-element.54), channel_id=1, source_target_pairs={{0,3},{1,0},{2,1},{3,2},{4,7},{5,4},{6,5},{7,6},{8,11},{9,8},{10,9... | collective-permute-start | bytes 786440 | tf_op jit(solution)/shard_map/ppermute | solution.py:357

commit v5 on v3

v5 whole, which is shorter than its diff:
```python
import jax
import jax.numpy as jnp
from jax import lax
from jax.experimental import pallas as pl
from jax.experimental.pallas import tpu as pltpu
from jax.sharding import Mesh
from jax.sharding import PartitionSpec as P


DK = 256
DV = 512
SPAN = 64
LANE = 128
SEQ = ("chip_x", "chip_z", "core")
CHIPS = ("chip_x", "chip_z")
F32 = jnp.float32
BF16 = jnp.bfloat16
VMEM = pl.BlockSpec(memory_space=pltpu.VMEM)
HBM = pl.BlockSpec(memory_space=pltpu.HBM)


def call(body, outs, *args, fetched=(), scratch=(), copies=0, outs_in=VMEM):
    moved = sum(a.size * a.dtype.itemsize for a in args)
    args = [
        pltpu.with_memory_space_constraint(a, pltpu.HBM) if i in fetched else a
        for i, a in enumerate(args)
    ]
    if fetched and not copies:
        scratch = [pltpu.VMEM(args[i].shape, args[i].dtype) for i in fetched]
        copies = len(fetched)
    if copies:
        scratch = [*scratch, pltpu.SemaphoreType.DMA((copies,))]
    return pl.pallas_call(
        body,
        out_shape=outs,
        in_specs=[HBM if i in fetched else VMEM for i in range(len(args))],
        out_specs=jax.tree.map(lambda _: outs_in, outs),
        scratch_shapes=scratch,
        cost_estimate=pl.CostEstimate(flops=10**9, transcendentals=0, bytes_accessed=moved),
        compiler_params=pltpu.CompilerParams(vmem_limit_bytes=16 * 2**20),
    )(*args)


def dot(a, b, dims=((1,), (0,))):
    return lax.dot_general(a, b, (dims, ((), ())), preferred_element_type=F32)


def triangle(length, keep):
    row = lax.broadcasted_iota(jnp.int32, (length, length), 0)
    col = lax.broadcasted_iota(jnp.int32, (length, length), 1)
    return jnp.where(keep(row, col), 1.0, 0.0).astype(BF16)


def stacked(*parts):
    row = lax.broadcasted_iota(jnp.int32, (8, LANE), 0)
    block = jnp.zeros((8, LANE), F32)
    for at, part in enumerate(parts):
        block = jnp.where(row == at, part, block)
    return block


def split_bf16(values):
    high = values.astype(BF16).astype(F32)
    return high, values - high


def fetch(sems, *pairs):
    copies = [pltpu.make_async_copy(src, dst, sems.at[i]) for i, (src, dst) in enumerate(pairs)]
    for copy in copies:
        copy.start()
    return copies


def columns(index, width):
    return pl.ds(pl.multiple_of(index * width, width), width)


def head_columns(shift, width):
    count = lax.axis_size("head")
    return columns(lax.rem(lax.axis_index("head") + shift, count), width)


def swap_body(k_hbm, v_hbm, g_hbm, swap_ref, log_ref, state_ref, k_ref, v_ref, g_ref, sems):
    gate_copy, k_copy, v_copy = fetch(sems, (g_hbm, g_ref), (k_hbm, k_ref), (v_hbm, v_ref))
    length = k_ref.shape[0]
    half = DV // 2
    mask = triangle(length, lambda r, c: c > r)
    gate_copy.wait()
    gate = g_ref[...]
    after = dot(mask, gate)
    total = after[0:1] + gate[0:1].astype(F32)
    k_copy.wait()
    k_state = (k_ref[...].astype(F32) * jnp.exp(after)).astype(BF16)
    state_ref[...] = k_state
    v_copy.wait()
    theirs = columns(1 - lax.axis_index("core"), half)
    state = dot(v_ref[:, theirs], k_state, ((0,), (0,))).astype(BF16)
    swap_ref[0:half, :] = state[:, :LANE]
    swap_ref[half : 2 * half, :] = state[:, LANE:]
    left_high, left_low = split_bf16(total[:, :LANE])
    right_high, right_low = split_bf16(total[:, LANE:])
    tail = stacked(left_high, right_high, left_low, right_low)
    swap_ref[2 * half :, :] = jnp.concatenate([tail, tail], axis=0).astype(BF16)
    log_ref[...] = stacked(total[:, :LANE], total[:, LANE:])


def own_body(v_hbm, state_ref, own_ref, v_ref, sems):
    (copy,) = fetch(sems, (v_hbm, v_ref))
    copy.wait()
    half = DV // 2
    mine = columns(lax.axis_index("core"), half)
    state = dot(v_ref[:, mine], state_ref[...], ((0,), (0,)))
    own_ref[0:half, :] = state[:, :LANE]
    own_ref[half:, :] = state[:, LANE:]


def join_body(own_ref, log_ref, swap_ref, out_ref, first_ref, decay_ref):
    pieces, rows = (out_ref.shape[0], (out_ref.shape[1] - 8) // 2)
    half = pieces * rows
    early = lax.axis_index("core") == 0
    tail = swap_ref[2 * half : 2 * half + 8, :].astype(F32)
    sums = []
    decays = []
    for side in range(2):
        at = slice(side * half, (side + 1) * half)
        own_log = log_ref[side : side + 1, :]
        other_log = tail[side : side + 1] + tail[side + 2 : side + 3]
        own = own_ref[at, :]
        other = swap_ref[at, :].astype(F32)
        first = jnp.where(early, own, other)
        second = jnp.where(early, other, own)
        state = first * jnp.exp(jnp.where(early, other_log, own_log)) + second
        first_ref[at, :] = first.astype(BF16)
        decays.append(jnp.exp(jnp.where(early, own_log, other_log)))
        sums.append(own_log + other_log)
        piece = slice(side * rows, (side + 1) * rows)
        out_ref[:, piece, :] = state.reshape(pieces, rows, LANE).astype(BF16)
    decay_ref[...] = stacked(*decays)
    left_high, left_low = split_bf16(sums[0])
    right_high, right_low = split_bf16(sums[1])
    tail = stacked(left_high, right_high, left_low, right_low)
    out_ref[:, 2 * rows :, :] = jnp.broadcast_to(tail[None], (pieces, 8, LANE)).astype(BF16)


def scan_body(in_ref, out_ref):
    pieces, rows = (in_ref.shape[0], out_ref.shape[1] // 2)
    left = right = jnp.zeros((rows, LANE), F32)
    for j in range(pieces):
        out_ref[j, 0:rows, :] = left.astype(BF16)
        out_ref[j, rows : 2 * rows, :] = right.astype(BF16)
        tail = in_ref[j, 2 * rows :, :].astype(F32)
        left = left * jnp.exp(tail[0:1] + tail[2:3]) + in_ref[j, 0:rows, :].astype(F32)
        right = right * jnp.exp(tail[1:2] + tail[3:4]) + in_ref[j, rows : 2 * rows, :].astype(F32)


def part_body(in_ref, first_ref, decay_ref, keep_ref, send_ref):
    pieces, rows = (in_ref.shape[0], in_ref.shape[1] // 2)
    half = pieces * rows
    early = lax.axis_index("core") == 0
    for side in range(2):
        at = slice(side * half, (side + 1) * half)
        piece = slice(side * rows, (side + 1) * rows)
        entering = in_ref[:, piece, :].astype(F32).reshape(half, LANE)
        between = entering * decay_ref[side : side + 1, :] + first_ref[at, :].astype(F32)
        keep_ref[at, :] = jnp.where(early, entering, between).astype(BF16)
        send_ref[at, :] = jnp.where(early, between, entering).astype(BF16)


def local_body(
    q_hbm, k_hbm, v_hbm, g_hbm, outer_hbm, gain_ref, att_ref, start_ref, scale_ref,
    q_ref, k_ref, v_ref, g_ref, outer_ref, sems,
):
    copies = fetch(
        sems, (g_hbm, g_ref), (q_hbm, q_ref), (k_hbm, k_ref), (v_hbm, v_ref), (outer_hbm, outer_ref)
    )
    length = q_ref.shape[0]
    lower = triangle(SPAN, lambda r, c: c <= r)
    row = lax.broadcasted_iota(jnp.int32, (SPAN, SPAN), 0)
    col = lax.broadcasted_iota(jnp.int32, (SPAN, SPAN), 1)
    for copy in copies:
        copy.wait()
    carried = None
    before = jnp.zeros((1, DK), F32)
    for i in range(length // SPAN):
        at = slice(i * SPAN, (i + 1) * SPAN)
        running = dot(lower, g_ref[at, :])
        middle = running[SPAN // 2 : SPAN // 2 + 1]
        ending = running[SPAN - 1 : SPAN]
        query_f = q_ref[at, :].astype(F32)
        key_f = k_ref[at, :].astype(F32)
        value = v_ref[at, :]
        q_inter = query_f * jnp.exp(running)
        q_intra = (query_f * jnp.exp(running - middle)).astype(BF16)
        k_intra = (key_f * jnp.exp(middle - running)).astype(BF16)
        scores = dot(q_intra, k_intra, ((1,), (1,)))
        weights = jnp.where(col <= row, scores, 0.0).astype(BF16)
        attention = dot(weights, value)
        if i:
            attention = attention + dot(q_inter.astype(BF16), carried.astype(BF16))
        att_ref[at, :] = attention
        start_ref[at, :] = (query_f * jnp.exp(running + before)).astype(BF16)
        before = before + ending
        if (i + 1) * SPAN < length:
            k_state = (key_f * jnp.exp(ending - running)).T.astype(BF16)
            block = dot(k_state, value)
            carried = block if i == 0 else carried * jnp.exp(ending).reshape(DK, 1) + block
        outer_f = outer_ref[at, :].astype(F32)
        scale = outer_f / (1.0 + jnp.exp(-outer_f)) * gain_ref[...]
        scale_ref[at, :] = scale.astype(BF16)


def finish_body(keep_ref, other_ref, q_ref, att_ref, scale_ref, top_ref, low_ref):
    half = DV // 2
    core = lax.axis_index("core")
    total = 0.0
    parts = []
    for ref, place in ((keep_ref, core), (other_ref, 1 - core)):
        attention = att_ref[:, columns(place, half)]
        attention = attention + dot(q_ref[:, :LANE], ref[:half, :], ((1,), (1,)))
        attention = attention + dot(q_ref[:, LANE:], ref[half:, :], ((1,), (1,)))
        total = total + jnp.sum(attention * attention, axis=-1, keepdims=True)
        parts.append((attention, place))
    inverse = lax.rsqrt(total * (1.0 / DV) + 1e-05)
    rows = top_ref.shape[0]
    for attention, place in parts:
        at = columns(place, half)
        gated = (attention * inverse * scale_ref[:, at].astype(F32)).astype(BF16)
        top_ref[:, at] = gated[:rows]
        low_ref[:, at] = gated[rows:]


def weights_body(w_hbm, *refs):
    out_refs, sems = (refs[:-1], refs[-1])
    width = out_refs[0].shape[1]
    for copy in fetch(
        sems,
        *((w_hbm.at[:, head_columns(i + 1, width)], ref) for i, ref in enumerate(out_refs)),
    ):
        copy.wait()


def own_part_body(top_ref, low_ref, w_hbm, out_ref, w_ref, sems):
    (copy,) = fetch(sems, (w_hbm.at[:, head_columns(0, w_ref.shape[1])], w_ref))
    copy.wait()
    rows = top_ref.shape[0]
    out_ref[:rows, :] = dot(top_ref[...], w_ref[...])
    out_ref[rows:, :] = dot(low_ref[...], w_ref[...])


def near_part_body(
    part_ref, below_top_ref, below_low_ref, above_top_ref, above_low_ref,
    w_below_hbm, w_above_hbm, out_ref, w_below_ref, w_above_ref, sems,
):
    below_copy, above_copy = fetch(sems, (w_below_hbm, w_below_ref), (w_above_hbm, w_above_ref))
    below_copy.wait()
    above_copy.wait()
    rows = below_top_ref.shape[0]
    for at, below, above in (
        (slice(0, rows), below_top_ref, above_top_ref),
        (slice(rows, 2 * rows), below_low_ref, above_low_ref),
    ):
        total = part_ref[at, :] + dot(below[...], w_below_ref[...])
        out_ref[at, :] = total + dot(above[...], w_above_ref[...])


def sum_body(part_ref, far_top_ref, far_low_ref, w_ref, out_ref):
    rows = far_top_ref.shape[0]
    out_ref[:rows, :] = (part_ref[:rows, :] + dot(far_top_ref[...], w_ref[...])).astype(BF16)
    out_ref[rows:, :] = (part_ref[rows:, :] + dot(far_low_ref[...], w_ref[...])).astype(BF16)


def ring(axis, shift):
    length = lax.axis_size(axis)
    return [(i, (i + shift) % length) for i in range(length)]


def shards(queries, key_vectors, values, log_gate, out_gate, norm_gain, out_weight):
    length = queries.shape[0]
    pieces = lax.axis_size(CHIPS)
    half = DV // 2
    rows = half // pieces
    width = out_weight.shape[1] // lax.axis_size("head")
    shape = jax.ShapeDtypeStruct
    small = shape((8, LANE), F32)
    swap, own_log, k_state = call(
        swap_body,
        (shape((DV + 16, LANE), BF16), small, shape((length, DK), BF16)),
        key_vectors,
        values,
        log_gate,
        fetched=(0, 1, 2),
    )
    swapped = lax.ppermute(swap, "core", ring("core", 1))
    own = call(own_body, shape((DV, LANE), F32), values, k_state, fetched=(0,))
    sent, first, decay = call(
        join_body,
        (shape((pieces, 2 * rows + 8, LANE), BF16), shape((DV, LANE), BF16), small),
        own,
        own_log,
        swapped,
    )
    sent, later_weight = lax.optimization_barrier((sent, out_weight))
    slices = lax.all_to_all(sent, CHIPS, 0, 0, tiled=True)
    blocks = call(
        weights_body,
        tuple(pltpu.HBM((DV, width), BF16) for _ in range(3)),
        later_weight,
        fetched=(0,),
        copies=3,
        outs_in=HBM,
    )
    up, down = ring("head", 1), ring("head", -1)
    w_below = lax.ppermute(blocks[0], "head", up)
    w_far = lax.ppermute(blocks[1], "head", ring("head", 2))
    w_above = lax.ppermute(blocks[2], "head", down)
    prefixes = call(scan_body, shape((pieces, 2 * rows, LANE), BF16), slices)
    prefixes, queries = lax.optimization_barrier((prefixes, queries))
    att_local, q_start, scale = call(
        local_body,
        (shape((length, DV), F32), shape((length, DK), BF16), shape((length, DV), BF16)),
        queries,
        key_vectors,
        values,
        log_gate,
        out_gate,
        norm_gain.reshape(1, DV),
        fetched=(0, 1, 2, 3, 4),
    )
    entering = lax.all_to_all(prefixes, CHIPS, 0, 0, tiled=True)
    state_half = shape((DV, LANE), BF16)
    entering, att_local, q_start, scale = lax.optimization_barrier(
        (entering, att_local, q_start, scale)
    )
    keep, send = call(part_body, (state_half, state_half), entering, first, decay)
    other = lax.ppermute(send, "core", ring("core", 1))
    near = shape((length // 2, DV), BF16)
    top, low = call(finish_body, (near, near), keep, other, q_start, att_local, scale)
    below_top = lax.ppermute(top, "head", up)
    above_low = lax.ppermute(low, "head", down)
    below_low = lax.ppermute(low, "head", up)
    above_top = lax.ppermute(top, "head", down)
    whole = shape((length, width), F32)
    part = call(
        own_part_body,
        whole,
        top,
        low,
        out_weight,
        fetched=(2,),
        scratch=[pltpu.VMEM((DV, width), BF16)],
        copies=1,
    )
    far_top = lax.ppermute(below_top, "head", up)
    far_low = lax.ppermute(above_low, "head", down)
    part = call(
        near_part_body,
        whole,
        part,
        below_top,
        below_low,
        above_top,
        above_low,
        w_below,
        w_above,
        fetched=(5, 6),
    )
    return call(sum_body, shape((length, width), BF16), part, far_top, far_low, w_far)


def solution(mesh):
    split = Mesh(mesh.devices.reshape(4, 8, 2, mesh.shape["head"]), (*SEQ, "head"))
    in_specs = (
        P(SEQ, "head"),
        P(SEQ, "head"),
        P(SEQ, "head"),
        P(SEQ, "head"),
        P(SEQ, "head"),
        P("head"),
        P("head", None),
    )
    out_specs = P(SEQ, "head")


    return jax.shard_map(
        shards, mesh=split, in_specs=in_specs, out_specs=out_specs, check_vma=False
    )
```

time: 74 us -> 125 us (1.69)
  Pallas kernels: 8.19 us -> 62.8 us
  blocking collectives: 37.3 us -> 23.3 us
  starting transfers between devices: 4.39 us -> 12.9 us
  waiting for transfers between devices: 20.7 us -> 24.1 us
  local copies, waits for them, and re-layouts: 2.98 us -> 0.87 us
    pallas_call x9 -> x11, Pallas kernels: 8.19 us -> 62.8 us  [call(): pl.pallas_call(body, out_shape=outs, in_specs=[HBM if i in fetched else V...]
    all_to_all x1 -> x0, blocking collectives: 14.5 us -> none  [shards(): entering = lax.all_to_all(prefixes, CHIPS, 0, 0, tiled=True)]
    ppermute x4 -> x9, waiting for transfers between devices: 19.4 us -> 24.1 us  [the longest x1 10.5 us: shards(): w_above = lax.ppermute(blocks[2], 'head', down)]
    ppermute x4 -> x9, starting transfers between devices: 4.21 us -> 8.69 us  [the longest x1 2.27 us: shards(): below_top = lax.ppermute(top, 'head', up)]
    all_to_all x0 -> x1, starting transfers between devices: none -> 4.04 us  [shards(): entering = lax.all_to_all(prefixes, CHIPS, 0, 0, tiled=True)]
    unnamed x20 -> x8, local copies, waits for them, and re-layouts: 2.98 us -> 0.87 us
    ppermute x1, waiting for transfers between devices: 1.34 us -> 0.01 us  [shards(): swapped = lax.ppermute(swap, 'core', ring('core', 1))]
  transfers between devices with their start and end apart: 6 -> 12, of which waited for: 5 -> 7; matrix products, arithmetic and copies ran while one was open for 0% -> 0% of each run, Pallas kernels for 6% -> 48%
where the time goes in v5:
time: 125 us; the launch traced here: 124 us
  Pallas kernels  62.8 us (50%)
  waiting for transfers between devices  24.1 us (19%)
  blocking collectives  23.3 us (19%)
  starting transfers between devices  12.9 us (10%)
    pallas_call x11, Pallas kernels, call(): pl.pallas_call(body, out_shape=outs, in_specs=[HBM if i in fetched else V...  62.8 us
    all_to_all x1, blocking collectives, shards(): slices = lax.all_to_all(sent, CHIPS, 0, 0, tiled=True)  23.3 us
    ppermute x1, waiting for transfers between devices, shards(): w_above = lax.ppermute(blocks[2], 'head', down)  10.5 us
    ppermute x1, waiting for transfers between devices, shards(): below_top = lax.ppermute(top, 'head', up)  5.36 us
    all_to_all x1, starting transfers between devices, shards(): entering = lax.all_to_all(prefixes, CHIPS, 0, 0, tiled=True)  4.04 us
    ppermute x1, waiting for transfers between devices, shards(): w_below = lax.ppermute(blocks[0], 'head', up)  2.99 us
  transfers between devices with their start and end apart: 12, of which 7 were waited for; matrix products, arithmetic and copies ran while one was open for 0% of the time, Pallas kernels for 48%

profile of v5, /device:TPU:24, one launch (start us, length us, event | category | flops | bytes accessed | tf_op | source)
XLA Modules:
  0.0 124.2 jit_solution(2053834264980142373)
XLA Ops:
  0.0 1.8 %shard_map.73 = (bf16[528,128]{1,0:T(8,128)(2,1)S(1)}, f32[8,128]{1,0:T(8,128)S(1)}, bf16[512,256]{1,0:T(8,128)(2,1)S(1)}) custom-call(bf16[512,256]{1,0:T(8,128)(2,1)} %k_hbm.3, bf16[512,512]{1,0:T(8,128)(2,1)} %v_hbm.5, bf16[512,256]{1,0:T(8,128)(2,1)} %g_hbm.3), custom_call_target="tpu_custom_call" | custom-call | flops 1000000000 | bytes 1048576 | tf_op jit(solution)/shard_map/pallas_call | solution.py:33
  1.9 1.3 %shard_map.74.own_ref = f32[512,128]{1,0:T(8,128)S(1)} custom-call(bf16[512,512]{1,0:T(8,128)(2,1)} %v_hbm.5, bf16[512,256]{1,0:T(8,128)(2,1)S(1)} %get-tuple-element.29.state_ref), custom_call_target="tpu_custom_call" | custom-call | flops 1000000000 | bytes 786432 | tf_op jit(solution)/shard_map/pallas_call | solution.py:33
  3.3 23.3 %all_to_all.10.in_ref = bf16[32,24,128]{2,1,0:T(8,128)(2,1)S(1)} all-to-all(bf16[32,24,128]{2,1,0:T(8,128)(2,1)S(1)} %get-tuple-element.33), channel_id=1, replica_groups=mesh['chip_x'=4,'chip_z'=8,'core'=2,'head'=4] {'chip_x','chip_z'}, dimensions={0} | all-to-all | bytes 393216 | tf_op jit(solution)/shard_map/all_to_all | solution.py:303
  26.6 0.7 shard_map.76
  27.4 4.0 %all-to-all-start.1 = ((bf16[32,16,128]{2,1,0:T(8,128)(2,1)}), bf16[32,16,128]{2,1,0:T(8,128)(2,1)S(1)}, u32[]{:S(2)}, u32[]{:S(2)}) async-start(bf16[32,16,128]{2,1,0:T(8,128)(2,1)} %shard_map.76), calls=%async_computation.1 | async-start | bytes 262144 | tf_op jit(solution)/shard_map/all_to_all | solution.py:329
  31.4 48.8 %shard_map.81 = (bf16[512,512]{1,0:T(8,128)(2,1)}, bf16[512,512]{1,0:T(8,128)(2,1)}, bf16[512,512]{1,0:T(8,128)(2,1)}) custom-call(bf16[512,2048]{1,0:T(8,128)(2,1)} %w_hbm.2), custom_call_target="tpu_custom_call" | custom-call | flops 1000000000 | bytes 2097152 | tf_op jit(solution)/shard_map/pallas_call | solution.py:33
  80.5 1.8 %collective-permute-start.7 = (bf16[512,512]{1,0:T(8,128)(2,1)}, bf16[512,512]{1,0:T(8,128)(2,1)S(1)}, u32[]{:S(2)}, u32[]{:S(2)}) collective-permute-start(bf16[512,512]{1,0:T(8,128)(2,1)} %get-tuple-element.51), channel_id=1, source_target_pairs={{0,3},{1,0},{2,1},{3,2},{4,7},{5,4},{6,5},{7,6},{8,11},{9,8},{10,9... | collective-permute-start | bytes 1572872 | tf_op jit(solution)/shard_map/ppermute | solution.py:315
  82.3 4.8 %shard_map.77 = (f32[512,512]{1,0:T(8,128)S(1)}, bf16[512,256]{1,0:T(8,128)(2,1)S(1)}, bf16[512,512]{1,0:T(8,128)(2,1)S(1)}) custom-call(bf16[512,256]{1,0:T(8,128)(2,1)} %q_hbm, bf16[512,256]{1,0:T(8,128)(2,1)} %k_hbm.3, bf16[512,512]{1,0:T(8,128)(2,1)} %v_hbm.5, bf16[512,256]{1,0:T(8,128)(2,1)} %g_hbm.3, bf16[512,512]{1,0:T(8,128)(2,1)} %outer_hbm.1, ...), custom_call_target="tpu_custom_call" | custom-call | flops 1000000000 | bytes 1837056 | tf_op jit(solution)/shard_map/pallas_call | solution.py:33
  87.3 0.9 copy-done.3
  88.2 1.2 collective-permute-start.10
  89.4 0.6 shard_map.79
  90.0 2.3 %collective-permute-start.2 = (bf16[256,512]{1,0:T(8,128)(2,1)S(1)}, bf16[256,512]{1,0:T(8,128)(2,1)S(1)}, u32[]{:S(2)}, u32[]{:S(2)}) collective-permute-start(bf16[256,512]{1,0:T(8,128)(2,1)S(1)} %get-tuple-element.47.top_ref), channel_id=1, source_target_pairs={{0,1},{1,2},{2,3},{3,0},{4,5},{5,6},{6,7},{7,4},{8,9},{9,10},{10,1... | collective-permute-start | bytes 786440 | tf_op jit(solution)/shard_map/ppermute | solution.py:338
  92.3 3.0 %collective-permute-done.6.w_below_hbm = bf16[512,512]{1,0:T(8,128)(2,1)S(1)} collective-permute-done((bf16[512,512]{1,0:T(8,128)(2,1)}, bf16[512,512]{1,0:T(8,128)(2,1)S(1)}, u32[]{:S(2)}, u32[]{:S(2)}) %collective-permute-start.6) | collective-permute-done | bytes 524320 | tf_op jit(solution)/shard_map/ppermute | solution.py:313
  95.8 10.5 %collective-permute-done.7.w_above_hbm = bf16[512,512]{1,0:T(8,128)(2,1)S(1)} collective-permute-done((bf16[512,512]{1,0:T(8,128)(2,1)}, bf16[512,512]{1,0:T(8,128)(2,1)S(1)}, u32[]{:S(2)}, u32[]{:S(2)}) %collective-permute-start.7) | collective-permute-done | bytes 524320 | tf_op jit(solution)/shard_map/ppermute | solution.py:315
  106.2 0.6 collective-permute-start.4
  106.8 5.4 %collective-permute-done.2.below_top_ref = bf16[256,512]{1,0:T(8,128)(2,1)S(1)} collective-permute-done((bf16[256,512]{1,0:T(8,128)(2,1)S(1)}, bf16[256,512]{1,0:T(8,128)(2,1)S(1)}, u32[]{:S(2)}, u32[]{:S(2)}) %collective-permute-start.2) | collective-permute-done | bytes 262176 | tf_op jit(solution)/shard_map/ppermute | solution.py:338
  112.2 0.5 collective-permute-start.8
  112.7 1.6 %collective-permute-start.9 = (bf16[256,512]{1,0:T(8,128)(2,1)S(1)}, bf16[256,512]{1,0:T(8,128)(2,1)S(1)}, u32[]{:S(2)}, u32[]{:S(2)}) collective-permute-start(bf16[256,512]{1,0:T(8,128)(2,1)S(1)} %collective-permute-done.5.above_low_ref), channel_id=1, source_target_pairs={{0,3},{1,0},{2,1},{3,2},{4,7},{5,4},{6,5},{7,6},{8,11},{9,8},{10,9... | collective-permute-start | bytes 786440 | tf_op jit(solution)/shard_map/ppermute | solution.py:354
  114.2 1.5 %shard_map.80.part_ref = f32[512,512]{1,0:T(8,128)S(1)} custom-call(bf16[256,512]{1,0:T(8,128)(2,1)S(1)} %get-tuple-element.47.top_ref, bf16[256,512]{1,0:T(8,128)(2,1)S(1)} %get-tuple-element.48.low_ref, bf16[512,2048]{1,0:T(8,128)(2,1)} %w_hbm.2), custom_call_target="tpu_custom_call" | custom-call | flops 1000000000 | bytes 2621440 | tf_op jit(solution)/shard_map/pallas_call | solution.py:33
  115.7 2.1 %collective-permute-done.3.below_low_ref = bf16[256,512]{1,0:T(8,128)(2,1)S(1)} collective-permute-done((bf16[256,512]{1,0:T(8,128)(2,1)S(1)}, bf16[256,512]{1,0:T(8,128)(2,1)S(1)}, u32[]{:S(2)}, u32[]{:S(2)}) %collective-permute-start.3) | collective-permute-done | bytes 262176 | tf_op jit(solution)/shard_map/ppermute | solution.py:340
  118.3 1.9 %shard_map.82.part_ref = f32[512,512]{1,0:T(8,128)S(1)} custom-call(f32[512,512]{1,0:T(8,128)S(1)} %shard_map.80.part_ref, bf16[256,512]{1,0:T(8,128)(2,1)S(1)} %collective-permute-done.2.below_top_ref, bf16[256,512]{1,0:T(8,128)(2,1)S(1)} %collective-permute-done.3.below_low_ref, bf16[256,512]{1,0:T(8,128)(2,1)S(1)} %collective-permute-done.4.above_top_ref, ...), custom_call_target="tpu_custom_call" | custom-call | flops 1000000000 | bytes 3145728 | tf_op jit(solution)/shard_map/pallas_call | solution.py:33
  120.2 1.5 %collective-permute-done.8.far_top_ref = bf16[256,512]{1,0:T(8,128)(2,1)S(1)} collective-permute-done((bf16[256,512]{1,0:T(8,128)(2,1)S(1)}, bf16[256,512]{1,0:T(8,128)(2,1)S(1)}, u32[]{:S(2)}, u32[]{:S(2)}) %collective-permute-start.8) | collective-permute-done | bytes 262176 | tf_op jit(solution)/shard_map/ppermute | solution.py:353
  121.7 1.3 %collective-permute-done.9.far_low_ref = bf16[256,512]{1,0:T(8,128)(2,1)S(1)} collective-permute-done((bf16[256,512]{1,0:T(8,128)(2,1)S(1)}, bf16[256,512]{1,0:T(8,128)(2,1)S(1)}, u32[]{:S(2)}, u32[]{:S(2)}) %collective-permute-start.9) | collective-permute-done | bytes 262176 | tf_op jit(solution)/shard_map/ppermute | solution.py:354
  123.0 1.2 shard_map.83
  (20 shorter events, 1.6 us)
Async XLA Ops:
  1.8 1.4 %collective-permute-start = (bf16[528,128]{1,0:T(8,128)(2,1)S(1)}, bf16[528,128]{1,0:T(8,128)(2,1)S(1)}, u32[]{:S(2)}, u32[]{:S(2)}) collective-permute-start(bf16[528,128]{1,0:T(8,128)(2,1)S(1)} %get-tuple-element.31), channel_id=1, source_target_pairs={{0,4},{4,0},{1,5},{5,1},{2,6},{6,2},{3,7},{7,3},{8,12},{12,8},{9,1... | collective-permute-start | bytes 405512 | tf_op jit(solution)/shard_map/ppermute | solution.py:293
  27.4 54.9 %copy-start = (f32[512]{0:T(512)S(1)}, f32[512]{0:T(512)}, u32[]{:S(2)}) copy-start(f32[512]{0:T(512)} %param.12) | copy-start | bytes 6148
  27.4 59.8 %all-to-all-start.1 = ((bf16[32,16,128]{2,1,0:T(8,128)(2,1)}), bf16[32,16,128]{2,1,0:T(8,128)(2,1)S(1)}, u32[]{:S(2)}, u32[]{:S(2)}) async-start(bf16[32,16,128]{2,1,0:T(8,128)(2,1)} %shard_map.76), calls=%async_computation.1 | async-start | bytes 262144 | tf_op jit(solution)/shard_map/all_to_all | solution.py:329
  80.2 15.1 %collective-permute-start.6 = (bf16[512,512]{1,0:T(8,128)(2,1)}, bf16[512,512]{1,0:T(8,128)(2,1)S(1)}, u32[]{:S(2)}, u32[]{:S(2)}) collective-permute-start(bf16[512,512]{1,0:T(8,128)(2,1)} %get-tuple-element.50), channel_id=1, source_target_pairs={{0,1},{1,2},{2,3},{3,0},{4,5},{5,6},{6,7},{7,4},{8,9},{9,10},{10,1... | collective-permute-start | bytes 1572872 | tf_op jit(solution)/shard_map/ppermute | solution.py:313
  80.5 25.7 %collective-permute-start.7 = (bf16[512,512]{1,0:T(8,128)(2,1)}, bf16[512,512]{1,0:T(8,128)(2,1)S(1)}, u32[]{:S(2)}, u32[]{:S(2)}) collective-permute-start(bf16[512,512]{1,0:T(8,128)(2,1)} %get-tuple-element.51), channel_id=1, source_target_pairs={{0,3},{1,0},{2,1},{3,2},{4,7},{5,4},{6,5},{7,6},{8,11},{9,8},{10,9... | collective-permute-start | bytes 1572872 | tf_op jit(solution)/shard_map/ppermute | solution.py:315
  87.2 1.0 copy-start.3
  87.2 2.2 %collective-permute-start.1 = (bf16[512,128]{1,0:T(8,128)(2,1)S(1)}, bf16[512,128]{1,0:T(8,128)(2,1)S(1)}, u32[]{:S(2)}, u32[]{:S(2)}) collective-permute-start(bf16[512,128]{1,0:T(8,128)(2,1)S(1)} %get-tuple-element.43), channel_id=1, source_target_pairs={{0,4},{4,0},{1,5},{5,1},{2,6},{6,2},{3,7},{7,3},{8,12},{12,8},{9,1... | collective-permute-start | bytes 393224 | tf_op jit(solution)/shard_map/ppermute | solution.py:335
  88.2 32.0 %collective-permute-start.10 = (bf16[512,512]{1,0:T(8,128)(2,1)S(1)}, bf16[512,512]{1,0:T(8,128)(2,1)S(1)}, u32[]{:S(2)}, u32[]{:S(2)}) collective-permute-start(bf16[512,512]{1,0:T(8,128)(2,1)S(1)} %copy-done.3), channel_id=1, source_target_pairs={{0,2},{1,3},{2,0},{3,1},{4,6},{5,7},{6,4},{7,5},{8,10},{9,11},{10,... | collective-permute-start | bytes 1572872 | tf_op jit(solution)/shard_map/ppermute | solution.py:314
  90.0 22.2 %collective-permute-start.2 = (bf16[256,512]{1,0:T(8,128)(2,1)S(1)}, bf16[256,512]{1,0:T(8,128)(2,1)S(1)}, u32[]{:S(2)}, u32[]{:S(2)}) collective-permute-start(bf16[256,512]{1,0:T(8,128)(2,1)S(1)} %get-tuple-element.47.top_ref), channel_id=1, source_target_pairs={{0,1},{1,2},{2,3},{3,0},{4,5},{5,6},{6,7},{7,4},{8,9},{9,10},{10,1... | collective-permute-start | bytes 786440 | tf_op jit(solution)/shard_map/ppermute | solution.py:338
  92.3 20.4 %collective-permute-start.5 = (bf16[256,512]{1,0:T(8,128)(2,1)S(1)}, bf16[256,512]{1,0:T(8,128)(2,1)S(1)}, u32[]{:S(2)}, u32[]{:S(2)}) collective-permute-start(bf16[256,512]{1,0:T(8,128)(2,1)S(1)} %get-tuple-element.48.low_ref), channel_id=1, source_target_pairs={{0,3},{1,0},{2,1},{3,2},{4,7},{5,4},{6,5},{7,6},{8,11},{9,8},{10,9... | collective-permute-start | bytes 786440 | tf_op jit(solution)/shard_map/ppermute | solution.py:339
  95.3 23.0 %copy-start.1 = (bf16[512,512]{1,0:T(8,128)(2,1)}, bf16[512,512]{1,0:T(8,128)(2,1)S(1)}, u32[]{:S(2)}) copy-start(bf16[512,512]{1,0:T(8,128)(2,1)S(1)} %collective-permute-done.6.w_below_hbm) | copy-start | bytes 1572868
  95.3 22.5 %collective-permute-start.3 = (bf16[256,512]{1,0:T(8,128)(2,1)S(1)}, bf16[256,512]{1,0:T(8,128)(2,1)S(1)}, u32[]{:S(2)}, u32[]{:S(2)}) collective-permute-start(bf16[256,512]{1,0:T(8,128)(2,1)S(1)} %get-tuple-element.48.low_ref), channel_id=1, source_target_pairs={{0,1},{1,2},{2,3},{3,0},{4,5},{5,6},{6,7},{7,4},{8,9},{9,10},{10,1... | collective-permute-start | bytes 786440 | tf_op jit(solution)/shard_map/ppermute | solution.py:340
  106.2 12.0 %copy-start.2 = (bf16[512,512]{1,0:T(8,128)(2,1)}, bf16[512,512]{1,0:T(8,128)(2,1)S(1)}, u32[]{:S(2)}) copy-start(bf16[512,512]{1,0:T(8,128)(2,1)S(1)} %collective-permute-done.7.w_above_hbm) | copy-start | bytes 1572868
  106.2 12.0 %collective-permute-start.4 = (bf16[256,512]{1,0:T(8,128)(2,1)S(1)}, bf16[256,512]{1,0:T(8,128)(2,1)S(1)}, u32[]{:S(2)}, u32[]{:S(2)}) collective-permute-start(bf16[256,512]{1,0:T(8,128)(2,1)S(1)} %get-tuple-element.47.top_ref), channel_id=1, source_target_pairs={{0,3},{1,0},{2,1},{3,2},{4,7},{5,4},{6,5},{7,6},{8,11},{9,8},{10,9... | collective-permute-start | bytes 786440 | tf_op jit(solution)/shard_map/ppermute | solution.py:341
  112.2 9.5 %collective-permute-start.8 = (bf16[256,512]{1,0:T(8,128)(2,1)S(1)}, bf16[256,512]{1,0:T(8,128)(2,1)S(1)}, u32[]{:S(2)}, u32[]{:S(2)}) collective-permute-start(bf16[256,512]{1,0:T(8,128)(2,1)S(1)} %collective-permute-done.2.below_top_ref), channel_id=1, source_target_pairs={{0,1},{1,2},{2,3},{3,0},{4,5},{5,6},{6,7},{7,4},{8,9},{9,10},{10,1... | collective-permute-start | bytes 786440 | tf_op jit(solution)/shard_map/ppermute | solution.py:353
  112.7 10.3 %collective-permute-start.9 = (bf16[256,512]{1,0:T(8,128)(2,1)S(1)}, bf16[256,512]{1,0:T(8,128)(2,1)S(1)}, u32[]{:S(2)}, u32[]{:S(2)}) collective-permute-start(bf16[256,512]{1,0:T(8,128)(2,1)S(1)} %collective-permute-done.5.above_low_ref), channel_id=1, source_target_pairs={{0,3},{1,0},{2,1},{3,2},{4,7},{5,4},{6,5},{7,6},{8,11},{9,8},{10,9... | collective-permute-start | bytes 786440 | tf_op jit(solution)/shard_map/ppermute | solution.py:354
